TPU v7x, 128 devices: a whole 4x4x4 slice. The times are simulated.
128 devices in a mesh: tp: 2 (over core), dp: 64 (over z, y, x).
Axes of the slice: x: 4, y: 4, z: 4, core: 2. Of those that a mesh axis runs over, the one named last changes fastest.
Arguments:
- hidden: bfloat16 [64, 512, 6144], P('dp')
- gain_in: float32 [6144], replicated
- gain_q: float32 [1536], replicated
- gain_kv: float32 [512], replicated
- w_qa: bfloat16 [6144, 1536], replicated
- w_kva: bfloat16 [6144, 576], replicated
- w_qb: bfloat16 [1536, 12288], P(None, 'tp')
- w_kvb: bfloat16 [512, 16384], P(None, 'tp')
- w_out: bfloat16 [8192, 6144], P('tp')
Outputs:
- output 1: bfloat16 [64, 512, 6144], P('dp')
- output 2: float32 [64], replicated
- output 3: bfloat16 [1536, 12288], P(None, 'tp')
- output 4: bfloat16 [512, 16384], P(None, 'tp')
All inputs are finite; a program needn't handle non-finite values.
Results may differ from a plain program's by a relative error of at most 0.00727773.
Values sent between devices are 32-bit elements.
A program may use at most 1 GiB of HBM per device.

v0:
```python
import math
import jax
import jax.numpy as jnp
from jax import lax
from jax.experimental import pallas as pl
from jax.experimental.pallas import tpu as pltpu
from jax.sharding import PartitionSpec as P

NORM_EPS = 1e-6
ROPE_BASE = 50000.0
MSCALE_SQ = (0.1 * math.log(32.0) + 1.0) ** 2
CLIP_TAU = 100.0
NOPE, ROPE, VDIM = 128, 64, 128
QK = NOPE + ROPE
LOGIT_SCALE = QK ** -0.5 * MSCALE_SQ
EXP2_SCALE = LOGIT_SCALE * math.log2(math.e)
GROUP = 4
NEG = -jnp.inf
MESH = pl.DeviceIdType.MESH
VMEM_MAX = 63 * 1024 * 1024
f32, bf16 = jnp.float32, jnp.bfloat16


def rope_tables(seq_len):
    inv_freq = ROPE_BASE ** (-2.0 * jnp.arange(ROPE // 2, dtype=f32) / ROPE)
    angles = jnp.arange(seq_len).astype(f32)[:, None] * inv_freq[None, :]
    cos, sin = jnp.cos(angles), jnp.sin(angles)
    one, zero = jnp.ones((seq_len, ROPE), f32), jnp.zeros((seq_len, ROPE), f32)
    half = jnp.zeros_like(sin)
    keep, low, high = (cos, cos), (-sin, half), (half, sin)
    first = [jnp.concatenate([*t, pad], axis=1) for t, pad in ((keep, one), (low, zero), (high, zero))]
    second = [jnp.concatenate([pad, *t], axis=1) for t, pad in ((keep, one), (low, zero), (high, zero))]
    return jnp.stack(first + second)


def turn(tensor, tables, start):
    return tensor * tables[start] + pltpu.roll(tensor, 96, 1) * tables[start + 1] + pltpu.roll(tensor, 32, 1) * tables[start + 2]


def latent_kernel(x_ref, gin_ref, gq_ref, gkv_ref, wqa_ref, wkva_ref, tab_ref, qlat_ref, lat_ref, kr_ref, scale_ref, accq_ref, acckv_ref):
    step, steps = pl.program_id(0), pl.num_programs(0)
    depth = wqa_ref.shape[0]
    rows, dim = x_ref.shape

    @pl.when(step == 0)
    def _():
        for r in range(0, rows, 64):
            total = jnp.zeros((64, 128), f32)
            for c in range(0, dim, 128):
                v = x_ref[r:r + 64, c:c + 128].astype(f32)
                total = total + v * v
            mean = jnp.sum(total, axis=1, keepdims=True) * (1.0 / dim)
            scale_ref[r:r + 64, :] = jnp.broadcast_to(lax.rsqrt(mean + NORM_EPS), (64, 128))

    start = pl.multiple_of(step * depth, depth)
    n = (x_ref[:, pl.ds(start, depth)].astype(f32) * scale_ref[:, 0:1] * gin_ref[:, pl.ds(start, depth)]).astype(bf16)
    pq = jnp.dot(n, wqa_ref[...], preferred_element_type=f32)
    pkv = jnp.dot(n, wkva_ref[...], preferred_element_type=f32)

    @pl.when(step == 0)
    def _():
        accq_ref[...] = pq
        acckv_ref[...] = pkv

    @pl.when(step > 0)
    def _():
        accq_ref[...] += pq
        acckv_ref[...] += pkv

    @pl.when(step == steps - 1)
    def _():
        q = accq_ref[...]
        qlat_ref[...] = (q * lax.rsqrt(jnp.mean(q * q, axis=1, keepdims=True) + NORM_EPS) * gq_ref[...]).astype(bf16)
        rank = lat_ref.shape[1]
        a = acckv_ref[:, :rank]
        lat_ref[...] = (a * lax.rsqrt(jnp.mean(a * a, axis=1, keepdims=True) + NORM_EPS) * gkv_ref[...]).astype(bf16)
        key = jnp.concatenate([acckv_ref[:, rank:rank + ROPE], jnp.zeros((rows, ROPE), f32)], axis=1)
        key = turn(key, tab_ref, 0)
        kr_ref[0] = key.astype(bf16)
        kr_ref[1] = pltpu.roll(key, 64, 1).astype(bf16)


def latents(x, gin, gq, gkv, wqa, wkva, tables):
    rows, dim = x.shape
    q_rank, kva, rank = wqa.shape[1], wkva.shape[1], gkv.shape[1]
    depth = 768
    whole = lambda shape: pl.BlockSpec(shape, lambda k: (0,) * len(shape), pipeline_mode=pl.Buffered(1))
    return pl.pallas_call(
        latent_kernel,
        grid=(dim // depth,),
        in_specs=[whole(x.shape), whole(gin.shape), whole(gq.shape), whole(gkv.shape), pl.BlockSpec((depth, q_rank), lambda k: (k, 0)), pl.BlockSpec((depth, kva), lambda k: (k, 0)), whole(tables.shape)],
        out_specs=[whole((rows, q_rank)), whole((rows, rank)), whole((2, rows, 128))],
        out_shape=[jax.ShapeDtypeStruct((rows, q_rank), bf16), jax.ShapeDtypeStruct((rows, rank), bf16), jax.ShapeDtypeStruct((2, rows, 128), bf16)],
        scratch_shapes=[pltpu.VMEM((rows, 128), f32), pltpu.VMEM((rows, q_rank), f32), pltpu.VMEM((rows, kva), f32)],
        compiler_params=pltpu.CompilerParams(vmem_limit_bytes=VMEM_MAX),
        name="latents",
    )(x, gin, gq, gkv, wqa, wkva, tables)


def attend(q, key, value, out_ref, column):
    rows = q.shape[0]
    block = 256
    best = None
    for b in range(rows // block):
        lo, hi = b * block, (b + 1) * block
        raw = lax.dot_general(q[lo:hi], key[:hi], (((1,), (1,)), ((), ())), preferred_element_type=f32)
        keep = lax.broadcasted_iota(jnp.int32, (block, block), 0) >= lax.broadcasted_iota(jnp.int32, (block, block), 1)
        last = jnp.where(keep, raw[:, lo:hi], NEG)
        raw = last if b == 0 else jnp.concatenate([raw[:, :lo], last], axis=1)
        top = jnp.max(raw, axis=1, keepdims=True)
        e = jnp.exp2(raw * EXP2_SCALE - top * EXP2_SCALE)
        p = (e * (1.0 / jnp.sum(e, axis=1, keepdims=True))).astype(bf16)
        out_ref[lo:hi, column:column + VDIM] = jnp.dot(p, value[:hi], preferred_element_type=f32).astype(bf16)
        peak = jnp.max(top, axis=0, keepdims=True)
        best = peak if best is None else jnp.maximum(best, peak)
    return best


def attention_kernel(qlat_ref, lat_ref, kr_ref, tab_ref, wqb_ref, wkvb_ref, o_ref, max_ref):
    group = pl.program_id(0)
    heads = pl.num_programs(0) * GROUP
    first = lax.axis_index("tp") * heads + group * GROUP
    q_all = jnp.dot(qlat_ref[...], wqb_ref[...], preferred_element_type=f32)
    kv_all = jnp.dot(lat_ref[...], wkvb_ref[...], preferred_element_type=f32)
    rows = q_all.shape[0]
    lane = lax.broadcasted_iota(jnp.int32, (rows, 128), 1)
    slot = lax.broadcasted_iota(jnp.int32, (8, 128), 1)

    @pl.when(group == 0)
    def _():
        max_ref[...] = jnp.full((8, 128), NEG, f32)

    found = max_ref[...]
    for pair in range(GROUP // 2):
        qc, kc = pair * 2 * QK, pair * 2 * (NOPE + VDIM)
        part_a = q_all[:, qc:qc + 128].astype(bf16)
        part_b = turn(q_all[:, qc + 128:qc + 256], tab_ref, 0).astype(bf16)
        part_c = turn(q_all[:, qc + 256:qc + 384], tab_ref, 3).astype(bf16)
        for odd in range(2):
            kcol = kc + odd * (NOPE + VDIM)
            nope = kv_all[:, kcol:kcol + NOPE]
            value = kv_all[:, kcol + NOPE:kcol + NOPE + VDIM].astype(bf16)
            if odd:
                moved = pltpu.roll(nope, 64, 1)
                q = jnp.concatenate([part_b, part_c], axis=1)
                key = jnp.concatenate([jnp.where(lane >= 64, moved, 0.0).astype(bf16), jnp.where(lane < 64, moved.astype(bf16), kr_ref[1])], axis=1)
            else:
                q = jnp.concatenate([part_a, part_b], axis=1)
                key = jnp.concatenate([nope.astype(bf16), kr_ref[0]], axis=1)
            best = attend(q, key, value, o_ref, (pair * 2 + odd) * VDIM)
            found = jnp.where(slot == first + pair * 2 + odd, best * LOGIT_SCALE, found)
    max_ref[...] = found


def attention(qlat, lat, kr, tables, wqb, wkvb):
    rows = qlat.shape[0]
    heads = wqb.shape[1] // QK
    whole = lambda shape: pl.BlockSpec(shape, lambda g: (0,) * len(shape), pipeline_mode=pl.Buffered(1))
    return pl.pallas_call(
        attention_kernel,
        grid=(heads // GROUP,),
        in_specs=[whole(qlat.shape), whole(lat.shape), whole(kr.shape), whole(tables.shape), pl.BlockSpec((wqb.shape[0], GROUP * QK), lambda g: (0, g)), pl.BlockSpec((wkvb.shape[0], GROUP * (NOPE + VDIM)), lambda g: (0, g))],
        out_specs=[pl.BlockSpec((rows, GROUP * VDIM), lambda g: (0, g)), pl.BlockSpec((8, 128), lambda g: (0, 0))],
        out_shape=[jax.ShapeDtypeStruct((rows, heads * VDIM), bf16), jax.ShapeDtypeStruct((8, 128), f32)],
        compiler_params=pltpu.CompilerParams(vmem_limit_bytes=VMEM_MAX),
        name="attention",
    )(qlat, lat, kr, tables, wqb, wkvb)


def axis_peers(axis):
    dp = lax.axis_index("dp")
    stride = 4 ** axis
    here = lax.rem(dp // stride, 4)
    return [dp + (lax.rem(here + d, 4) - here) * stride for d in (1, 2, 3)]


def output_kernel(blocks, o_ref, w_ref, x_ref, max_ref, y_ref, top_ref, part, recv, best, peer_best, send_sem, recv_sem, max_send, max_recv):
    step = pl.program_id(0)
    tp, dp = lax.axis_index("tp"), lax.axis_index("dp")
    other = (1 - tp, dp)

    def exchange(index):
        return pltpu.make_async_remote_copy(
            src_ref=part.at[lax.rem(index, 3)], dst_ref=recv.at[index], send_sem=send_sem.at[lax.rem(index, 3)], recv_sem=recv_sem.at[index], device_id=other, device_id_type=MESH
        )

    def spread(phase, slot, device):
        return pltpu.make_async_remote_copy(
            src_ref=max_ref if phase == 0 else best.at[phase - 1], dst_ref=peer_best.at[slot], send_sem=max_send.at[slot], recv_sem=max_recv.at[slot], device_id=device, device_id_type=MESH
        )

    def phase_copies(phase):
        if phase == 0:
            return [spread(0, 0, other)]
        return [spread(phase, 1 + 3 * (phase - 1) + d, (tp, peer)) for d, peer in enumerate(axis_peers(phase - 1))]

    @pl.when(step == 0)
    def _():
        barrier = pltpu.get_barrier_semaphore()
        peers = [other] + [(tp, peer) for axis in range(3) for peer in axis_peers(axis)]
        for peer in peers:
            pl.semaphore_signal(barrier, inc=1, device_id=peer, device_id_type=MESH)
        pl.semaphore_wait(barrier, len(peers))

    for phase in range(4):
        @pl.when(step == 3 * phase)
        def _():
            for copy in phase_copies(phase):
                copy.start()

        @pl.when(step == 3 * phase + 2)
        def _():
            value = max_ref[...] if phase == 0 else best[phase - 1]
            copies = phase_copies(phase)
            slots = [0] if phase == 0 else [1 + 3 * (phase - 1) + d for d in range(3)]
            for copy, slot in zip(copies, slots):
                copy.wait()
                value = jnp.maximum(value, peer_best[slot])
            if phase < 3:
                best[phase] = value
            else:
                top_ref[...] = value

    def finish(index):
        y_ref[...] = (x_ref[...].astype(f32) + (part[lax.rem(index, 3)] + recv[index])).astype(bf16)

    def multiply():
        part[lax.rem(step, 3)] = jnp.dot(o_ref[...], w_ref[...], preferred_element_type=f32)

    @pl.when(step >= 2)
    def _():
        exchange(step - 2).wait()

    @pl.when(step < 2)
    def _():
        multiply()

    @pl.when((step >= 2) & (step < blocks))
    def _():
        multiply()
        finish(step - 2)

    @pl.when(step >= blocks)
    def _():
        finish(step - 2)

    @pl.when(step < blocks)
    def _():
        exchange(step).start()


def output_projection(o, w_out, x, local_max):
    rows, depth = o.shape
    dim = w_out.shape[1]
    width = 512
    blocks = dim // width
    whole = lambda shape: pl.BlockSpec(shape, lambda j: (0,) * len(shape), pipeline_mode=pl.Buffered(1))
    late = pl.BlockSpec((rows, width), lambda j: (0, jnp.maximum(j - 2, 0)))
    return pl.pallas_call(
        lambda *refs: output_kernel(blocks, *refs),
        grid=(blocks + 2,),
        in_specs=[whole(o.shape), pl.BlockSpec((depth, width), lambda j: (0, jnp.minimum(j, blocks - 1))), late, whole((8, 128))],
        out_specs=[late, whole((8, 128))],
        out_shape=[jax.ShapeDtypeStruct((rows, dim), bf16), jax.ShapeDtypeStruct((8, 128), f32)],
        scratch_shapes=[
            pltpu.VMEM((3, rows, width), f32),
            pltpu.VMEM((blocks, rows, width), f32),
            pltpu.VMEM((3, 8, 128), f32),
            pltpu.VMEM((10, 8, 128), f32),
            pltpu.SemaphoreType.DMA((3,)),
            pltpu.SemaphoreType.DMA((blocks,)),
            pltpu.SemaphoreType.DMA((10,)),
            pltpu.SemaphoreType.DMA((10,)),
        ],
        compiler_params=pltpu.CompilerParams(vmem_limit_bytes=VMEM_MAX, collective_id=0, has_side_effects=True),
        name="output_projection",
    )(o, w_out, x, local_max)


def clip_kernel(top_ref, wqb_ref, wkvb_ref, nqb_ref, nkvb_ref):
    group = pl.program_id(0)
    first = lax.axis_index("tp") * pl.num_programs(0) * GROUP + group * GROUP

    def gains(width, first_dim, second_is_clip):
        column = lax.broadcasted_iota(jnp.int32, (1, GROUP * width), 1)
        best, inner = jnp.full((1, GROUP * width), top_ref[0, first], f32), column
        for i in range(1, GROUP):
            best = jnp.where(column >= i * width, top_ref[0, first + i], best)
            inner = jnp.where(column >= i * width, column - i * width, inner)
        clip = CLIP_TAU / jnp.maximum(CLIP_TAU, best)
        return jnp.where(inner < first_dim, jnp.sqrt(clip), clip if second_is_clip else 1.0)

    nqb_ref[...] = (wqb_ref[...].astype(f32) * gains(QK, NOPE, True)).astype(bf16)
    nkvb_ref[...] = (wkvb_ref[...].astype(f32) * gains(NOPE + VDIM, NOPE, False)).astype(bf16)


def clip(top, wqb, wkvb):
    steps = wqb.shape[1] // (QK * GROUP)
    qspec = pl.BlockSpec((wqb.shape[0], GROUP * QK), lambda g: (0, g))
    kvspec = pl.BlockSpec((wkvb.shape[0], GROUP * (NOPE + VDIM)), lambda g: (0, g))
    return pl.pallas_call(
        clip_kernel,
        grid=(steps,),
        in_specs=[pl.BlockSpec(memory_space=pltpu.SMEM), qspec, kvspec],
        out_specs=[qspec, kvspec],
        out_shape=[jax.ShapeDtypeStruct(wqb.shape, bf16), jax.ShapeDtypeStruct(wkvb.shape, bf16)],
        compiler_params=pltpu.CompilerParams(vmem_limit_bytes=VMEM_MAX),
        name="clip",
    )(top, wqb, wkvb)


def solution(mesh):
    def device_step(hidden, gain_in, gain_q, gain_kv, w_qa, w_kva, w_qb, w_kvb, w_out):
        x = hidden[0]
        tables = rope_tables(x.shape[0])
        qlat, lat, kr = latents(x, gain_in[None], gain_q[None], gain_kv[None], w_qa, w_kva, tables)
        o, local_max = attention(qlat, lat, kr, tables, w_qb, w_kvb)
        y, top = output_projection(o, w_out, x, local_max)
        new_qb, new_kvb = clip(top, w_qb, w_kvb)
        return y[None], top[0, :64], new_qb, new_kvb

    weight_spec = P(None, 'tp')
    return jax.shard_map(device_step, mesh=mesh, in_specs=(P('dp', None, None), P(), P(), P(), P(), P(), weight_spec, weight_spec, P('tp', None)), out_specs=(P('dp', None, None), P(), weight_spec, weight_spec), check_vma=False)
```

profile of v0, /device:TPU:1, one launch (start us, length us, event | category | flops | bytes accessed | tf_op | source)
XLA Modules:
  0.0 170.5 jit_solution(15636030021285931250)
XLA Ops:
  0.7 1.3 broadcast_in_dim.24.gq_ref
  2.0 1.0 multiply_sine_fusion
  3.0 0.9 fusion.10
  3.9 0.9 fusion.7
  4.8 0.9 fusion.9
  5.8 0.9 fusion.11
  6.7 0.9 fusion.2
  7.6 0.9 fusion.5.tab_ref
  8.5 10.5 %copy.13.wkva_ref = bf16[6144,576]{1,0:T(8,128)(2,1)} copy(bf16[6144,576]{0,1:T(8,128)(2,1)} %param.14) | data formatting | bytes 14155776 | tf_op args[5]
  19.0 28.1 %latents.1 = (bf16[512,1536]{1,0:T(8,128)(2,1)}, bf16[512,512]{1,0:T(8,128)(2,1)}, bf16[2,512,128]{2,1,0:T(8,128)(2,1)}) custom-call(bf16[512,6144]{1,0:T(8,128)(2,1)} %bitcast.30, f32[1,6144]{1,0:T(1,128)} %bitcast.33, f32[1,1536]{1,0:T(1,128)} %broadcast_in_dim.24.gq_ref, f32[1,512]{1,0:T(1,128)} %bitcast.34, bf16[6144,1536]{1,0:T(8,128)(2,1)} %wqa_ref.1, ...), custom_call_target="tpu_custom_call" | custom-call | tf_op jit(solution)/shard_map/latents/pallas_call | solution.py:88
  47.1 50.7 %attention.1 = (bf16[512,4096]{1,0:T(8,128)(2,1)}, f32[8,128]{1,0:T(8,128)}) custom-call(bf16[512,1536]{1,0:T(8,128)(2,1)} %get-tuple-element.13.qlat_ref, bf16[512,512]{1,0:T(8,128)(2,1)} %get-tuple-element.14.lat_ref, bf16[2,512,128]{2,1,0:T(8,128)(2,1)} %get-tuple-element.15.kr_ref, f32[6,512,128]{2,1,0:T(8,128)} %fusion.5.tab_ref, ...), custom_call_target="tpu_custom_call" | custom-call | tf_op jit(solution)/shard_map/attention/pallas_call | solution.py:159
  97.8 45.4 %output_projection.1 = (bf16[512,6144]{1,0:T(8,128)(2,1)}, f32[8,128]{1,0:T(8,128)}) custom-call(bf16[512,4096]{1,0:T(8,128)(2,1)} %get-tuple-element.16.refs_0_, bf16[4096,6144]{1,0:T(8,128)(2,1)} %refs_1_.1, bf16[512,6144]{1,0:T(8,128)(2,1)} %bitcast.31, f32[8,128]{1,0:T(8,128)} %get-tuple-element.17.refs_3_), custom_call_target="tpu_custom_call" | custom-call | tf_op jit(solution)/shard_map/output_projection/pallas_call | solution.py:259
  143.2 1.2 slice_bitcast_fusion
  144.4 19.9 %clip.1 = (bf16[1536,6144]{1,0:T(8,128)(2,1)}, bf16[512,8192]{1,0:T(8,128)(2,1)}) custom-call(f32[8,128]{1,0:T(8,128)} %get-tuple-element.19.top_ref, bf16[1536,6144]{1,0:T(8,128)(2,1)} %wqb_ref.3, bf16[512,8192]{1,0:T(8,128)(2,1)} %wkvb_ref.3), custom_call_target="tpu_custom_call" | custom-call | tf_op jit(solution)/shard_map/clip/pallas_call | solution.py:301
  164.3 6.2 %copy.20 = bf16[1,512,6144]{2,1,0:T(8,128)(2,1)} copy(bf16[1,512,6144]{2,1,0:T(8,128)(2,1)} %bitcast.32) | data formatting | bytes 12582912
  (5 shorter events, 0.1 us)
where the time goes:
time: 171 us
  Pallas kernels  144 us (84%)
  local copies, waits for them, and re-layouts  19.2 us (11%)
  other arithmetic  6.46 us (4%)
    pallas_call x1, Pallas kernels, attention(): pl.pallas_call(attention_kernel, grid=(heads // GROUP,), in_specs=[whole(...  50.7 us
    pallas_call x1, Pallas kernels, output_projection(): pl.pallas_call(lambda *refs: output_kernel(blocks, *refs), grid=(blocks +...  45.4 us
    pallas_call x1, Pallas kernels, latents(): pl.pallas_call(latent_kernel, grid=(dim // depth,), in_specs=[whole(x.sha...  28.1 us
    pallas_call x1, Pallas kernels, clip(): pl.pallas_call(clip_kernel, grid=(steps,), in_specs=[pl.BlockSpec(memory_...  19.9 us
    unnamed x2, local copies, waits for them, and re-layouts  16.7 us
    unnamed x5, other arithmetic  4.55 us

commit v1 on v0

v1 whole, which is shorter than its diff:
```python
import math
import jax
import jax.numpy as jnp
import numpy as np
from jax import lax
from jax.experimental import pallas as pl
from jax.experimental.pallas import tpu as pltpu
from jax.sharding import PartitionSpec as P

NORM_EPS = 1e-6
ROPE_BASE = 50000.0
MSCALE_SQ = (0.1 * math.log(32.0) + 1.0) ** 2
CLIP_TAU = 100.0
NOPE, ROPE, VDIM = 128, 64, 128
QK = NOPE + ROPE
LOGIT_SCALE = QK ** -0.5 * MSCALE_SQ
EXP2_SCALE = LOGIT_SCALE * math.log2(math.e)
GROUP = 4
NEG = -jnp.inf
MESH = pl.DeviceIdType.MESH
VMEM_MAX = 63 * 1024 * 1024
f32, bf16 = jnp.float32, jnp.bfloat16


def rope_tables(seq_len):
    inv_freq = ROPE_BASE ** (-2.0 * np.arange(ROPE // 2) / ROPE)
    angles = np.arange(seq_len)[:, None] * inv_freq[None, :]
    cos, sin = np.cos(angles), np.sin(angles)
    half, rest = np.zeros_like(sin), np.zeros((seq_len, ROPE))
    return np.stack([np.concatenate(t, axis=1) for t in ((cos, cos, rest + 1.0), (-sin, half, rest), (half, sin, rest))]).astype(np.float32)


def turn(tensor, tables):
    return tensor * tables[0] + pltpu.roll(tensor, 96, 1) * tables[1] + pltpu.roll(tensor, 32, 1) * tables[2]


TILE = 256


def latent_kernel(x_hbm, gin_ref, gq_ref, gkv_ref, wqa_hbm, wkva_hbm, tab_ref, qlat_ref, lat_ref, kr_ref, x_ref, n_ref, wq_ref, wkv_ref, wr_ref, full_q, full_kv, rot, scale_ref, x_sem, w_sem, send_sem, recv_sem):
    rows, dim = x_ref.shape
    tp, dp = lax.axis_index("tp"), lax.axis_index("dp")
    other = (1 - tp, dp)
    tiles, parts = wq_ref.shape[0], rows // 128
    rank = lat_ref.shape[1]

    x_copies = [pltpu.make_async_copy(x_hbm.at[pl.ds(r * 128, 128)], x_ref.at[pl.ds(r * 128, 128)], x_sem.at[r]) for r in range(parts)]
    kv_copy = pltpu.make_async_copy(wkva_hbm.at[pl.ds(pl.multiple_of(tp * TILE, TILE), TILE)], wkv_ref, w_sem.at[tiles])
    r_copy = pltpu.make_async_copy(wkva_hbm.at[pl.ds(rank, ROPE)], wr_ref, w_sem.at[tiles + 1])
    q_copies = [pltpu.make_async_copy(wqa_hbm.at[:, pl.ds(pl.multiple_of((tp * tiles + i) * TILE, TILE), TILE)], wq_ref.at[i], w_sem.at[i]) for i in range(tiles)]
    for copy in [*x_copies, *q_copies, kv_copy, r_copy]:
        copy.start()
    barrier = pltpu.get_barrier_semaphore()
    pl.semaphore_signal(barrier, inc=1, device_id=other, device_id_type=MESH)

    def send(ref, index, slot):
        return pltpu.make_async_remote_copy(src_ref=ref.at[index], dst_ref=ref.at[index], send_sem=send_sem.at[slot], recv_sem=recv_sem.at[slot], device_id=other, device_id_type=MESH)

    half = rows // 2

    def measure(part):
        x_copies[2 * part].wait()
        x_copies[2 * part + 1].wait()

        @pl.loop(0, half // 32)
        def _(i):
            here = pl.ds(pl.multiple_of(part * half + i * 32, 32), 32)
            total = jnp.zeros((32, 256), f32)
            for c in range(0, dim, 256):
                v = x_ref[here, c:c + 256].astype(f32)
                total = total + v * v
            scale_ref[here] = jnp.broadcast_to(lax.rsqrt(jnp.sum(total, axis=1, keepdims=True) * (1.0 / dim) + NORM_EPS), (32, 128))

    def normalize(here):
        scale = scale_ref[here, 0:1]
        for c in range(0, dim, 256):
            n_ref[here, c:c + 256] = (x_ref[here, c:c + 256].astype(f32) * scale * gin_ref[:, c:c + 256]).astype(bf16)

    flip = (((1,), (1,)), ((), ()))
    upper, lower = slice(0, half), slice(half, rows)

    measure(0)

    @pl.loop(0, half // 32)
    def _(i):
        normalize(pl.ds(pl.multiple_of(i * 32, 32), 32))

    measure(1)
    q_copies[0].wait()
    q_copies[1].wait()
    for j in range(2):
        full_q[tp * tiles + j, upper] = jnp.dot(n_ref[upper], wq_ref[j], preferred_element_type=f32)
    for r in range(half, rows, 32):
        normalize(slice(r, r + 32))
    pl.semaphore_wait(barrier, 1)
    for j in range(2):
        full_q[tp * tiles + j, lower] = jnp.dot(n_ref[lower], wq_ref[j], preferred_element_type=f32)
    sends = [send(full_q, tp * tiles + j, j) for j in range(2)]
    for copy in sends:
        copy.start()
    q_copies[2].wait()
    for part in (upper, lower):
        full_q[tp * tiles + 2, part] = jnp.dot(n_ref[part], wq_ref[2], preferred_element_type=f32)
    sends.append(send(full_q, tp * tiles + 2, 2))
    sends[2].start()
    kv_copy.wait()
    r_copy.wait()
    for part in (upper, lower):
        full_kv[tp, part] = lax.dot_general(n_ref[part], wkv_ref[...], flip, preferred_element_type=f32)
    sends.append(send(full_kv, tp, tiles))
    sends[3].start()
    quarter = half // 2
    for i in range(2):
        mine = pl.ds(pl.multiple_of(tp * half + i * quarter, quarter), quarter)
        turned = lax.dot_general(n_ref[mine], wr_ref[...], flip, preferred_element_type=f32)
        rot[tp, i * quarter:i * quarter + quarter] = jnp.concatenate([turned, jnp.zeros((quarter, ROPE), f32)], axis=1)
    sends.append(send(rot, tp, tiles + 1))
    sends[4].start()
    for copy in sends[:3]:
        copy.wait()

    @pl.loop(0, rows // 32)
    def _(i):
        here = pl.ds(pl.multiple_of(i * 32, 32), 32)
        pieces = [full_q[j, here] for j in range(2 * tiles)]
        total = sum(a * a for a in pieces)
        scale = lax.rsqrt(jnp.sum(total, axis=1, keepdims=True) * (1.0 / (2 * tiles * TILE)) + NORM_EPS)
        for j, a in enumerate(pieces):
            qlat_ref[here, j * TILE:j * TILE + TILE] = (a * scale * gq_ref[:, j * TILE:j * TILE + TILE]).astype(bf16)

    for copy in sends[3:]:
        copy.wait()
    for r in range(0, rows, 64):
        here = slice(r, r + 64)
        pieces = [full_kv[j, here] for j in range(rank // TILE)]
        total = sum(a * a for a in pieces)
        scale = lax.rsqrt(jnp.sum(total, axis=1, keepdims=True) * (1.0 / rank) + NORM_EPS)
        for j, a in enumerate(pieces):
            lat_ref[here, j * TILE:j * TILE + TILE] = (a * scale * gkv_ref[:, j * TILE:j * TILE + TILE]).astype(bf16)
        key = turn(rot[r // half, r % half:r % half + 64], [tab_ref[i, here] for i in range(3)])
        kr_ref[0, here] = key.astype(bf16)
        kr_ref[1, here] = pltpu.roll(key, 64, 1).astype(bf16)


def latents(x, gin, gq, gkv, wqa, wkva, tables):
    rows, dim = x.shape
    q_rank, rank = wqa.shape[1], gkv.shape[1]
    tiles = q_rank // (2 * TILE)
    vmem, hbm = pl.BlockSpec(memory_space=pltpu.VMEM), pl.BlockSpec(memory_space=pl.ANY)
    return pl.pallas_call(
        latent_kernel,
        in_specs=[hbm, vmem, vmem, vmem, hbm, hbm, vmem],
        out_specs=[vmem, vmem, vmem],
        out_shape=[jax.ShapeDtypeStruct((rows, q_rank), bf16), jax.ShapeDtypeStruct((rows, rank), bf16), jax.ShapeDtypeStruct((2, rows, 128), bf16)],
        scratch_shapes=[
            pltpu.VMEM((rows, dim), bf16),
            pltpu.VMEM((rows, dim), bf16),
            pltpu.VMEM((tiles, dim, TILE), bf16),
            pltpu.VMEM((TILE, dim), bf16),
            pltpu.VMEM((ROPE, dim), bf16),
            pltpu.VMEM((2 * tiles, rows, TILE), f32),
            pltpu.VMEM((rank // TILE, rows, TILE), f32),
            pltpu.VMEM((2, rows // 2, 128), f32),
            pltpu.VMEM((rows, 128), f32),
            pltpu.SemaphoreType.DMA((rows // 128,)),
            pltpu.SemaphoreType.DMA((tiles + 2,)),
            pltpu.SemaphoreType.DMA((tiles + 2,)),
            pltpu.SemaphoreType.DMA((tiles + 2,)),
        ],
        compiler_params=pltpu.CompilerParams(vmem_limit_bytes=VMEM_MAX, collective_id=1, has_side_effects=True),
        name="latents",
    )(x, gin, gq, gkv, wqa, wkva, tables)


BLOCK, CHUNK = 256, 32


def attention_kernel(qlat_ref, lat_ref, kr_ref, tab_ref, wqb_ref, wkvb_ref, o_ref, max_ref, mirror, *scratch):
    step, steps = pl.program_id(0), pl.num_programs(0)
    sets = (scratch[0:3], scratch[3:6])
    raws, probs = scratch[6:10], scratch[10:14]
    heads = (steps - 1) * GROUP
    rows = qlat_ref.shape[0]
    lane = lax.broadcasted_iota(jnp.int32, (rows, 128), 1)

    @pl.when(step == 0)
    def _():
        max_ref[...] = jnp.full((8, 128), NEG, f32)
        for i in range(3):
            mirror[i] = pltpu.roll(tab_ref[i], 64, 1)
        for _, keys, _ in sets:
            for h in range(0, GROUP, 2):
                keys[:, h * 256 + 128:h * 256 + 256] = kr_ref[0]
        for i, prob in enumerate(probs):
            column = 128 + i % 2 * BLOCK
            prob[0:128, column:column + 128] = jnp.zeros((128, 128), bf16)

    def project_q(buffers, n):
        queries = buffers[0]
        chunk = jnp.dot(qlat_ref[...], wqb_ref[:, n * 256:n * 256 + 256], preferred_element_type=f32)
        for i in range(2):
            piece, kind = chunk[:, i * 128:i * 128 + 128], (2 * n + i) % 3
            if kind:
                piece = turn(piece, tab_ref if kind == 1 else mirror)
            queries[:, (2 * n + i) * 128:(2 * n + i) * 128 + 128] = piece.astype(bf16)

    def project_kv(buffers, h):
        _, keys, values = buffers
        chunk = jnp.dot(lat_ref[...], wkvb_ref[:, h * 256:h * 256 + 256], preferred_element_type=f32)
        values[:, h * VDIM:h * VDIM + VDIM] = chunk[:, NOPE:].astype(bf16)
        if h % 2:
            moved = pltpu.roll(chunk[:, :NOPE], 64, 1)
            keys[:, h * 256:h * 256 + 128] = jnp.where(lane >= 64, moved, 0.0).astype(bf16)
            keys[:, h * 256 + 128:h * 256 + 256] = jnp.where(lane < 64, moved.astype(bf16), kr_ref[1])
        else:
            keys[:, h * 256:h * 256 + 128] = chunk[:, :NOPE].astype(bf16)

    def scores(buffers, h):
        queries, keys, _ = buffers
        column = (h // 2) * 384 + (h % 2) * 128
        for b in range(2):
            hi = (b + 1) * BLOCK
            raws[2 * (h % 2) + b][:, :hi] = lax.dot_general(queries[b * BLOCK:hi, column:column + 256], keys[:hi, h * 256:h * 256 + 256], (((1,), (1,)), ((), ())), preferred_element_type=f32)

    def attend(buffers, h):
        values = buffers[2]
        peak = None
        for b in range(2):
            hi = (b + 1) * BLOCK
            raw, prob = raws[2 * (h % 2) + b], probs[2 * (h % 2) + b]
            for r in range(0, BLOCK, CHUNK):
                width = b * BLOCK + (r // 128 + 1) * 128
                tile = raw[r:r + CHUNK, :width]
                keep = lax.broadcasted_iota(jnp.int32, (CHUNK, 128), 0) + r % 128 >= lax.broadcasted_iota(jnp.int32, (CHUNK, 128), 1)
                last = jnp.where(keep, tile[:, width - 128:], NEG)
                tile = last if width == 128 else jnp.concatenate([tile[:, :width - 128], last], axis=1)
                top = jnp.max(tile, axis=1, keepdims=True)
                e = jnp.exp2(tile * EXP2_SCALE - top * EXP2_SCALE)
                prob[r:r + CHUNK, :width] = (e * (1.0 / jnp.sum(e, axis=1, keepdims=True))).astype(bf16)
                peak = top if peak is None else jnp.maximum(peak, top)
            o_ref[b * BLOCK:hi, h * VDIM:h * VDIM + VDIM] = jnp.dot(prob[:, :hi], values[:hi, h * VDIM:h * VDIM + VDIM], preferred_element_type=f32).astype(bf16)
        slot = lax.broadcasted_iota(jnp.int32, (8, 128), 1)
        index = lax.axis_index("tp") * heads + (step - 1) * GROUP + h
        max_ref[...] = jnp.where(slot == index, jnp.max(peak, axis=0, keepdims=True) * LOGIT_SCALE, max_ref[...])

    @pl.when(step == 0)
    def _():
        for n in range(3):
            project_q(sets[0], n)
        for h in range(GROUP):
            project_kv(sets[0], h)
        scores(sets[0], 0)

    for parity in range(2):
        for h in range(GROUP):
            @pl.when((step > 0) & (step < steps - 1) & (lax.rem(step, 2) == parity))
            def _():
                ahead, now = sets[parity], sets[1 - parity]
                if h < GROUP - 1:
                    project_q(ahead, h)
                    scores(now, h + 1)
                else:
                    for i in range(GROUP):
                        project_kv(ahead, i)
                    scores(ahead, 0)
                attend(now, h)

    @pl.when(step == steps - 1)
    def _():
        for h in range(GROUP):
            if h < GROUP - 1:
                scores(sets[1], h + 1)
            attend(sets[1], h)


def attention(qlat, lat, kr, tables, wqb, wkvb):
    rows = qlat.shape[0]
    heads = wqb.shape[1] // QK
    groups = heads // GROUP
    whole = lambda shape: pl.BlockSpec(shape, lambda g: (0,) * len(shape), pipeline_mode=pl.Buffered(1))
    ahead = lambda g: (0, jnp.minimum(g, groups - 1))
    buffers = [pltpu.VMEM((rows, GROUP * QK), bf16), pltpu.VMEM((rows, GROUP * 256), bf16), pltpu.VMEM((rows, GROUP * VDIM), bf16)]
    return pl.pallas_call(
        attention_kernel,
        grid=(groups + 1,),
        in_specs=[whole(qlat.shape), whole(lat.shape), whole(kr.shape), whole(tables.shape), pl.BlockSpec((wqb.shape[0], GROUP * QK), ahead), pl.BlockSpec((wkvb.shape[0], GROUP * (NOPE + VDIM)), ahead)],
        out_specs=[pl.BlockSpec((rows, GROUP * VDIM), lambda g: (0, jnp.maximum(g - 1, 0))), pl.BlockSpec((8, 128), lambda g: (0, 0))],
        out_shape=[jax.ShapeDtypeStruct((rows, heads * VDIM), bf16), jax.ShapeDtypeStruct((8, 128), f32)],
        scratch_shapes=[pltpu.VMEM(tables.shape, f32)] + buffers + buffers + [pltpu.VMEM((BLOCK, (1 + i % 2) * BLOCK), f32) for i in range(4)] + [pltpu.VMEM((BLOCK, (1 + i % 2) * BLOCK), bf16) for i in range(4)],
        compiler_params=pltpu.CompilerParams(vmem_limit_bytes=VMEM_MAX),
        name="attention",
    )(qlat, lat, kr, tables, wqb, wkvb)


def axis_peers(axis):
    dp = lax.axis_index("dp")
    stride = 4 ** axis
    here = lax.rem(dp // stride, 4)
    return [dp + (lax.rem(here + d, 4) - here) * stride for d in (1, 2, 3)]


def output_kernel(blocks, o_ref, w_ref, x_ref, max_ref, y_ref, top_ref, part, recv, best, peer_best, send_sem, recv_sem, max_send, max_recv):
    step = pl.program_id(0)
    tp, dp = lax.axis_index("tp"), lax.axis_index("dp")
    other = (1 - tp, dp)

    def exchange(index):
        return pltpu.make_async_remote_copy(
            src_ref=part.at[lax.rem(index, 3)], dst_ref=recv.at[index], send_sem=send_sem.at[lax.rem(index, 3)], recv_sem=recv_sem.at[index], device_id=other, device_id_type=MESH
        )

    def spread(phase, slot, device):
        return pltpu.make_async_remote_copy(
            src_ref=max_ref if phase == 0 else best.at[phase - 1], dst_ref=peer_best.at[slot], send_sem=max_send.at[slot], recv_sem=max_recv.at[slot], device_id=device, device_id_type=MESH
        )

    def phase_copies(phase):
        if phase == 0:
            return [spread(0, 0, other)]
        return [spread(phase, 1 + 3 * (phase - 1) + d, (tp, peer)) for d, peer in enumerate(axis_peers(phase - 1))]

    @pl.when(step == 0)
    def _():
        barrier = pltpu.get_barrier_semaphore()
        peers = [other] + [(tp, peer) for axis in range(3) for peer in axis_peers(axis)]
        for peer in peers:
            pl.semaphore_signal(barrier, inc=1, device_id=peer, device_id_type=MESH)
        pl.semaphore_wait(barrier, len(peers))

    for phase in range(4):
        @pl.when(step == 3 * phase)
        def _():
            for copy in phase_copies(phase):
                copy.start()

        @pl.when(step == 3 * phase + 2)
        def _():
            value = max_ref[...] if phase == 0 else best[phase - 1]
            copies = phase_copies(phase)
            slots = [0] if phase == 0 else [1 + 3 * (phase - 1) + d for d in range(3)]
            for copy, slot in zip(copies, slots):
                copy.wait()
                value = jnp.maximum(value, peer_best[slot])
            if phase < 3:
                best[phase] = value
            else:
                top_ref[...] = value

    def finish(index):
        y_ref[...] = (x_ref[...].astype(f32) + (part[lax.rem(index, 3)] + recv[index])).astype(bf16)

    def multiply():
        part[lax.rem(step, 3)] = jnp.dot(o_ref[...], w_ref[...], preferred_element_type=f32)
        exchange(step).start()

    @pl.when(step < 2)
    def _():
        multiply()

    @pl.when((step >= 2) & (step < blocks))
    def _():
        exchange(step - 2).wait()
        finish(step - 2)
        multiply()

    @pl.when(step >= blocks)
    def _():
        exchange(step - 2).wait()
        finish(step - 2)


def output_projection(o, w_out, x, local_max):
    rows, depth = o.shape
    dim = w_out.shape[1]
    width = 512
    blocks = dim // width
    whole = lambda shape: pl.BlockSpec(shape, lambda j: (0,) * len(shape), pipeline_mode=pl.Buffered(1))
    late = pl.BlockSpec((rows, width), lambda j: (0, jnp.maximum(j - 2, 0)))
    return pl.pallas_call(
        lambda *refs: output_kernel(blocks, *refs),
        grid=(blocks + 2,),
        in_specs=[whole(o.shape), pl.BlockSpec((depth, width), lambda j: (0, jnp.minimum(j, blocks - 1))), late, whole((8, 128))],
        out_specs=[late, whole((8, 128))],
        out_shape=[jax.ShapeDtypeStruct((rows, dim), bf16), jax.ShapeDtypeStruct((8, 128), f32)],
        scratch_shapes=[
            pltpu.VMEM((3, rows, width), f32),
            pltpu.VMEM((blocks, rows, width), f32),
            pltpu.VMEM((3, 8, 128), f32),
            pltpu.VMEM((10, 8, 128), f32),
            pltpu.SemaphoreType.DMA((3,)),
            pltpu.SemaphoreType.DMA((blocks,)),
            pltpu.SemaphoreType.DMA((10,)),
            pltpu.SemaphoreType.DMA((10,)),
        ],
        compiler_params=pltpu.CompilerParams(vmem_limit_bytes=VMEM_MAX, collective_id=0, has_side_effects=True),
        name="output_projection",
    )(o, w_out, x, local_max)


def clip_kernel(top_ref, wqb_ref, wkvb_ref, nqb_ref, nkvb_ref):
    group = pl.program_id(0)
    first = lax.axis_index("tp") * pl.num_programs(0) * GROUP + group * GROUP

    def gains(width, first_dim, second_is_clip):
        column = lax.broadcasted_iota(jnp.int32, (1, GROUP * width), 1)
        best, inner = jnp.full((1, GROUP * width), top_ref[0, first], f32), column
        for i in range(1, GROUP):
            best = jnp.where(column >= i * width, top_ref[0, first + i], best)
            inner = jnp.where(column >= i * width, column - i * width, inner)
        clip = CLIP_TAU / jnp.maximum(CLIP_TAU, best)
        return jnp.where(inner < first_dim, jnp.sqrt(clip), clip if second_is_clip else 1.0)

    nqb_ref[...] = (wqb_ref[...].astype(f32) * gains(QK, NOPE, True)).astype(bf16)
    nkvb_ref[...] = (wkvb_ref[...].astype(f32) * gains(NOPE + VDIM, NOPE, False)).astype(bf16)


def clip(top, wqb, wkvb):
    steps = wqb.shape[1] // (QK * GROUP)
    qspec = pl.BlockSpec((wqb.shape[0], GROUP * QK), lambda g: (0, g))
    kvspec = pl.BlockSpec((wkvb.shape[0], GROUP * (NOPE + VDIM)), lambda g: (0, g))
    return pl.pallas_call(
        clip_kernel,
        grid=(steps,),
        in_specs=[pl.BlockSpec(memory_space=pltpu.SMEM), qspec, kvspec],
        out_specs=[qspec, kvspec],
        out_shape=[jax.ShapeDtypeStruct(wqb.shape, bf16), jax.ShapeDtypeStruct(wkvb.shape, bf16)],
        compiler_params=pltpu.CompilerParams(vmem_limit_bytes=VMEM_MAX),
        name="clip",
    )(top, wqb, wkvb)


def solution(mesh):
    def device_step(hidden, gain_in, gain_q, gain_kv, w_qa, w_kva, w_qb, w_kvb, w_out):
        x = hidden[0]
        tables = rope_tables(x.shape[0])
        qlat, lat, kr = latents(x, gain_in[None], gain_q[None], gain_kv[None], w_qa, w_kva.T, tables)
        o, local_max = attention(qlat, lat, kr, tables, w_qb, w_kvb)
        y, top = output_projection(o, w_out, x, local_max)
        new_qb, new_kvb = clip(top, w_qb, w_kvb)
        return y[None], top[0, :64], new_qb, new_kvb

    weight_spec = P(None, 'tp')
    return jax.shard_map(device_step, mesh=mesh, in_specs=(P('dp', None, None), P(), P(), P(), P(), P(), weight_spec, weight_spec, P('tp', None)), out_specs=(P('dp', None, None), P(), weight_spec, weight_spec), check_vma=False)
```

time: 171 us -> 125 us (0.73)
  Pallas kernels: 144 us -> 115 us
  local copies, waits for them, and re-layouts: 19.2 us -> 8.72 us
  other arithmetic: 6.46 us -> 0 us
    pallas_call x2, Pallas kernels: 78.8 us -> 49.3 us  [the longest x1 27.9 us: attention(): pl.pallas_call(attention_kernel, grid=(groups + 1,), in_specs=[whole(qlat...]
    unnamed x2 -> x1, local copies, waits for them, and re-layouts: 16.7 us -> 6.23 us
    unnamed x5 -> x0, other arithmetic: 4.55 us -> none
where the time goes in v1:
time: 125 us; the launch traced here: 124 us
  Pallas kernels  115 us (92%)
  local copies, waits for them, and re-layouts  8.72 us (7%)
    pallas_call x1, Pallas kernels, output_projection(): pl.pallas_call(lambda *refs: output_kernel(blocks, *refs), grid=(blocks +...  45.8 us
    pallas_call x1, Pallas kernels, attention(): pl.pallas_call(attention_kernel, grid=(groups + 1,), in_specs=[whole(qlat...  27.9 us
    pallas_call x1, Pallas kernels, latents(): pl.pallas_call(latent_kernel, in_specs=[hbm, vmem, vmem, vmem, hbm, hbm,...  21.4 us
    pallas_call x1, Pallas kernels, clip(): pl.pallas_call(clip_kernel, grid=(steps,), in_specs=[pl.BlockSpec(memory_...  19.9 us
    unnamed x1, local copies, waits for them, and re-layouts  6.23 us

profile of v1, /device:TPU:1, one launch (start us, length us, event | category | flops | bytes accessed | tf_op | source)
XLA Modules:
  0.0 124.3 jit_solution(16789517903413151063)
XLA Ops:
  0.6 1.3 %broadcast_in_dim.13.gq_ref = f32[1,1536]{1,0:T(1,128)} reshape(f32[1536]{0:T(1024)} %param.12) | data formatting | bytes 12288 | tf_op jit(solution)/shard_map/broadcast_in_dim | solution.py:436
  1.9 21.4 %latents.1 = (bf16[512,1536]{1,0:T(8,128)(2,1)}, bf16[512,512]{1,0:T(8,128)(2,1)}, bf16[2,512,128]{2,1,0:T(8,128)(2,1)}) custom-call(bf16[512,6144]{1,0:T(8,128)(2,1)} %bitcast.7, f32[1,6144]{1,0:T(1,128)} %bitcast.11, f32[1,1536]{1,0:T(1,128)} %broadcast_in_dim.13.gq_ref, f32[1,512]{1,0:T(1,128)} %bitcast.12, bf16[6144,1536]{1,0:T(8,128)(2,1)} %wqa_hbm.1, ...), custom_call_target="tpu_custom_call" | custom-call | tf_op jit(solution)/shard_map/latents/pallas_call | solution.py:150
  23.3 27.9 %attention.1 = (bf16[512,4096]{1,0:T(8,128)(2,1)}, f32[8,128]{1,0:T(8,128)}) custom-call(bf16[512,1536]{1,0:T(8,128)(2,1)} %get-tuple-element.13.qlat_ref, bf16[512,512]{1,0:T(8,128)(2,1)} %get-tuple-element.14.lat_ref, bf16[2,512,128]{2,1,0:T(8,128)(2,1)} %get-tuple-element.15.kr_ref, f32[3,512,128]{2,1,0:T(8,128)} %constant.2.clone.tab_ref, ...), custom_call_target="tpu_custom_call" | custom-call | tf_op jit(solution)/shard_map/attention/pallas_call | solution.py:283
  51.2 45.8 %output_projection.1 = (bf16[512,6144]{1,0:T(8,128)(2,1)}, f32[8,128]{1,0:T(8,128)}) custom-call(bf16[512,4096]{1,0:T(8,128)(2,1)} %get-tuple-element.16.refs_0_, bf16[4096,6144]{1,0:T(8,128)(2,1)} %refs_1_.1, bf16[512,6144]{1,0:T(8,128)(2,1)} %bitcast.8, f32[8,128]{1,0:T(8,128)} %get-tuple-element.17.refs_3_), custom_call_target="tpu_custom_call" | custom-call | tf_op jit(solution)/shard_map/output_projection/pallas_call | solution.py:379
  97.0 1.2 slice_bitcast_fusion
  98.2 19.9 %clip.1 = (bf16[1536,6144]{1,0:T(8,128)(2,1)}, bf16[512,8192]{1,0:T(8,128)(2,1)}) custom-call(f32[8,128]{1,0:T(8,128)} %get-tuple-element.19.top_ref, bf16[1536,6144]{1,0:T(8,128)(2,1)} %wqb_ref.3, bf16[512,8192]{1,0:T(8,128)(2,1)} %wkvb_ref.3), custom_call_target="tpu_custom_call" | custom-call | tf_op jit(solution)/shard_map/clip/pallas_call | solution.py:421
  118.1 6.2 %copy.15 = bf16[1,512,6144]{2,1,0:T(8,128)(2,1)} copy(bf16[1,512,6144]{2,1,0:T(8,128)(2,1)} %bitcast.10) | data formatting | bytes 12582912

commit v2 on v1

--- a/solution.py
+++ b/solution.py
@@ -18,7 +18,7 @@
 GROUP = 4
 NEG = -jnp.inf
 MESH = pl.DeviceIdType.MESH
-VMEM_MAX = 63 * 1024 * 1024
+MIB = 1024 * 1024
 f32, bf16 = jnp.float32, jnp.bfloat16
 
 
@@ -28,6 +28,14 @@
     cos, sin = np.cos(angles), np.sin(angles)
     half, rest = np.zeros_like(sin), np.zeros((seq_len, ROPE))
     return np.stack([np.concatenate(t, axis=1) for t in ((cos, cos, rest + 1.0), (-sin, half, rest), (half, sin, rest))]).astype(np.float32)
+
+
+def in_vmem(array):
+    return pltpu.with_memory_space_constraint(array, pltpu.VMEM)
+
+
+def in_hbm(array):
+    return pltpu.with_memory_space_constraint(array, pltpu.HBM)
 
 
 def turn(tensor, tables):
@@ -126,7 +134,7 @@
         total = sum(a * a for a in pieces)
         scale = lax.rsqrt(jnp.sum(total, axis=1, keepdims=True) * (1.0 / (2 * tiles * TILE)) + NORM_EPS)
         for j, a in enumerate(pieces):
-            qlat_ref[here, j * TILE:j * TILE + TILE] = (a * scale * gq_ref[:, j * TILE:j * TILE + TILE]).astype(bf16)
+            qlat_ref[here, j * TILE:j * TILE + TILE] = (a * scale * jnp.concatenate([gq_ref[2 * j:2 * j + 1], gq_ref[2 * j + 1:2 * j + 2]], axis=1)).astype(bf16)
 
     for copy in sends[3:]:
         copy.wait()
@@ -146,12 +154,12 @@
     rows, dim = x.shape
     q_rank, rank = wqa.shape[1], gkv.shape[1]
     tiles = q_rank // (2 * TILE)
-    vmem, hbm = pl.BlockSpec(memory_space=pltpu.VMEM), pl.BlockSpec(memory_space=pl.ANY)
+    vmem, hbm = pl.BlockSpec(memory_space=pltpu.VMEM), pl.BlockSpec(memory_space=pltpu.HBM)
     return pl.pallas_call(
         latent_kernel,
         in_specs=[hbm, vmem, vmem, vmem, hbm, hbm, vmem],
         out_specs=[vmem, vmem, vmem],
-        out_shape=[jax.ShapeDtypeStruct((rows, q_rank), bf16), jax.ShapeDtypeStruct((rows, rank), bf16), jax.ShapeDtypeStruct((2, rows, 128), bf16)],
+        out_shape=[pltpu.VMEM((rows, q_rank), bf16), pltpu.VMEM((rows, rank), bf16), pltpu.VMEM((2, rows, 128), bf16)],
         scratch_shapes=[
             pltpu.VMEM((rows, dim), bf16),
             pltpu.VMEM((rows, dim), bf16),
@@ -167,21 +175,34 @@
             pltpu.SemaphoreType.DMA((tiles + 2,)),
             pltpu.SemaphoreType.DMA((tiles + 2,)),
         ],
-        compiler_params=pltpu.CompilerParams(vmem_limit_bytes=VMEM_MAX, collective_id=1, has_side_effects=True),
+        compiler_params=pltpu.CompilerParams(vmem_limit_bytes=32 * MIB, collective_id=1, has_side_effects=True),
         name="latents",
-    )(x, gin, gq, gkv, wqa, wkva, tables)
+    )(in_hbm(x), gin, gq, gkv, in_hbm(wqa), in_hbm(wkva), tables)
 
 
 BLOCK, CHUNK = 256, 32
 
 
-def attention_kernel(qlat_ref, lat_ref, kr_ref, tab_ref, wqb_ref, wkvb_ref, o_ref, max_ref, mirror, *scratch):
+def attention_kernel(qlat_ref, lat_ref, kr_ref, tab_ref, wqb_hbm, wkvb_ref, o_ref, wqb_ref, max_ref, w_sem, mirror, *scratch):
     step, steps = pl.program_id(0), pl.num_programs(0)
     sets = (scratch[0:3], scratch[3:6])
     raws, probs = scratch[6:10], scratch[10:14]
-    heads = (steps - 1) * GROUP
+    heads = o_ref.shape[1] // VDIM
     rows = qlat_ref.shape[0]
     lane = lax.broadcasted_iota(jnp.int32, (rows, 128), 1)
+
+    def fetch(group):
+        columns = pl.ds(pl.multiple_of(group * (GROUP * QK), 256), GROUP * QK)
+        return pltpu.make_async_copy(wqb_hbm.at[:, columns], wqb_ref.at[:, columns], w_sem.at[group])
+
+    @pl.when(step == 0)
+    def _():
+        for group in range(heads // GROUP):
+            fetch(group).start()
+
+    @pl.when(step < steps - 1)
+    def _():
+        fetch(step).wait()
 
     @pl.when(step == 0)
     def _():
@@ -197,7 +218,7 @@
 
     def project_q(buffers, n):
         queries = buffers[0]
-        chunk = jnp.dot(qlat_ref[...], wqb_ref[:, n * 256:n * 256 + 256], preferred_element_type=f32)
+        chunk = jnp.dot(qlat_ref[...], wqb_ref[:, pl.ds(pl.multiple_of(step * (GROUP * QK) + n * 256, 256), 256)], preferred_element_type=f32)
         for i in range(2):
             piece, kind = chunk[:, i * 128:i * 128 + 128], (2 * n + i) % 3
             if kind:
@@ -238,7 +259,7 @@
                 e = jnp.exp2(tile * EXP2_SCALE - top * EXP2_SCALE)
                 prob[r:r + CHUNK, :width] = (e * (1.0 / jnp.sum(e, axis=1, keepdims=True))).astype(bf16)
                 peak = top if peak is None else jnp.maximum(peak, top)
-            o_ref[b * BLOCK:hi, h * VDIM:h * VDIM + VDIM] = jnp.dot(prob[:, :hi], values[:hi, h * VDIM:h * VDIM + VDIM], preferred_element_type=f32).astype(bf16)
+            o_ref[b * BLOCK:hi, pl.ds(pl.multiple_of((step - 1) * (GROUP * VDIM) + h * VDIM, VDIM), VDIM)] = jnp.dot(prob[:, :hi], values[:hi, h * VDIM:h * VDIM + VDIM], preferred_element_type=f32).astype(bf16)
         slot = lax.broadcasted_iota(jnp.int32, (8, 128), 1)
         index = lax.axis_index("tp") * heads + (step - 1) * GROUP + h
         max_ref[...] = jnp.where(slot == index, jnp.max(peak, axis=0, keepdims=True) * LOGIT_SCALE, max_ref[...])
@@ -277,19 +298,18 @@
     rows = qlat.shape[0]
     heads = wqb.shape[1] // QK
     groups = heads // GROUP
-    whole = lambda shape: pl.BlockSpec(shape, lambda g: (0,) * len(shape), pipeline_mode=pl.Buffered(1))
-    ahead = lambda g: (0, jnp.minimum(g, groups - 1))
+    vmem, hbm = pl.BlockSpec(memory_space=pltpu.VMEM), pl.BlockSpec(memory_space=pltpu.HBM)
     buffers = [pltpu.VMEM((rows, GROUP * QK), bf16), pltpu.VMEM((rows, GROUP * 256), bf16), pltpu.VMEM((rows, GROUP * VDIM), bf16)]
     return pl.pallas_call(
         attention_kernel,
         grid=(groups + 1,),
-        in_specs=[whole(qlat.shape), whole(lat.shape), whole(kr.shape), whole(tables.shape), pl.BlockSpec((wqb.shape[0], GROUP * QK), ahead), pl.BlockSpec((wkvb.shape[0], GROUP * (NOPE + VDIM)), ahead)],
-        out_specs=[pl.BlockSpec((rows, GROUP * VDIM), lambda g: (0, jnp.maximum(g - 1, 0))), pl.BlockSpec((8, 128), lambda g: (0, 0))],
-        out_shape=[jax.ShapeDtypeStruct((rows, heads * VDIM), bf16), jax.ShapeDtypeStruct((8, 128), f32)],
-        scratch_shapes=[pltpu.VMEM(tables.shape, f32)] + buffers + buffers + [pltpu.VMEM((BLOCK, (1 + i % 2) * BLOCK), f32) for i in range(4)] + [pltpu.VMEM((BLOCK, (1 + i % 2) * BLOCK), bf16) for i in range(4)],
-        compiler_params=pltpu.CompilerParams(vmem_limit_bytes=VMEM_MAX),
+        in_specs=[vmem, vmem, vmem, vmem, hbm, pl.BlockSpec((wkvb.shape[0], GROUP * 256), lambda g: (0, jnp.minimum(g, groups - 1)))],
+        out_specs=[vmem, vmem, vmem],
+        out_shape=[pltpu.VMEM((rows, heads * VDIM), bf16), pltpu.VMEM(wqb.shape, bf16), pltpu.VMEM((8, 128), f32)],
+        scratch_shapes=[pltpu.SemaphoreType.DMA((groups,)), pltpu.VMEM(tables.shape, f32)] + buffers + buffers + [pltpu.VMEM((BLOCK, (1 + i % 2) * BLOCK), f32) for i in range(4)] + [pltpu.VMEM((BLOCK, (1 + i % 2) * BLOCK), bf16) for i in range(4)],
+        compiler_params=pltpu.CompilerParams(vmem_limit_bytes=15 * MIB),
         name="attention",
-    )(qlat, lat, kr, tables, wqb, wkvb)
+    )(in_vmem(qlat), in_vmem(lat), in_vmem(kr), tables, in_hbm(wqb), in_hbm(wkvb))
 
 
 def axis_peers(axis):
@@ -299,107 +319,151 @@
     return [dp + (lax.rem(here + d, 4) - here) * stride for d in (1, 2, 3)]
 
 
-def output_kernel(blocks, o_ref, w_ref, x_ref, max_ref, y_ref, top_ref, part, recv, best, peer_best, send_sem, recv_sem, max_send, max_recv):
-    step = pl.program_id(0)
+def output_kernel(o_ref, w_hbm, x_hbm, max_ref, y_ref, top_ref, o_buf, w_buf, part, recv, best, peer_best, x_sem, w_sem, send_sem, recv_sem, max_send, max_recv, free_sem):
+    slots, rows, width = recv.shape
+    blocks = y_ref.shape[1] // width
     tp, dp = lax.axis_index("tp"), lax.axis_index("dp")
     other = (1 - tp, dp)
 
+    def fetch(index):
+        slot = lax.rem(index, 2)
+        return pltpu.make_async_copy(w_hbm.at[:, pl.ds(pl.multiple_of(index * width, width), width)], w_buf.at[slot], w_sem.at[slot])
+
     def exchange(index):
-        return pltpu.make_async_remote_copy(
-            src_ref=part.at[lax.rem(index, 3)], dst_ref=recv.at[index], send_sem=send_sem.at[lax.rem(index, 3)], recv_sem=recv_sem.at[index], device_id=other, device_id_type=MESH
-        )
+        slot, place = lax.rem(index, 3), lax.rem(index, slots)
+        return pltpu.make_async_remote_copy(src_ref=part.at[slot], dst_ref=recv.at[place], send_sem=send_sem.at[slot], recv_sem=recv_sem.at[place], device_id=other, device_id_type=MESH)
 
     def spread(phase, slot, device):
         return pltpu.make_async_remote_copy(
             src_ref=max_ref if phase == 0 else best.at[phase - 1], dst_ref=peer_best.at[slot], send_sem=max_send.at[slot], recv_sem=max_recv.at[slot], device_id=device, device_id_type=MESH
         )
 
+    def phase_slots(phase):
+        return [0] if phase == 0 else [1 + 3 * (phase - 1) + d for d in range(3)]
+
     def phase_copies(phase):
-        if phase == 0:
-            return [spread(0, 0, other)]
-        return [spread(phase, 1 + 3 * (phase - 1) + d, (tp, peer)) for d, peer in enumerate(axis_peers(phase - 1))]
-
-    @pl.when(step == 0)
-    def _():
-        barrier = pltpu.get_barrier_semaphore()
-        peers = [other] + [(tp, peer) for axis in range(3) for peer in axis_peers(axis)]
-        for peer in peers:
-            pl.semaphore_signal(barrier, inc=1, device_id=peer, device_id_type=MESH)
-        pl.semaphore_wait(barrier, len(peers))
-
-    for phase in range(4):
-        @pl.when(step == 3 * phase)
+        devices = [other] if phase == 0 else [(tp, peer) for peer in axis_peers(phase - 1)]
+        return [spread(phase, slot, device) for slot, device in zip(phase_slots(phase), devices)]
+
+    def finish(index):
+        columns = pl.ds(pl.multiple_of(index * width, width), width)
+        for r in range(0, rows, 32):
+            here = slice(r, r + 32)
+            y_ref[here, columns] = (y_ref[here, columns].astype(f32) + (part[lax.rem(index, 3), here] + recv[lax.rem(index, slots), here])).astype(bf16)
+
+    def multiply(index):
+        part[lax.rem(index, 3)] = jnp.dot(o_buf[...], w_buf[lax.rem(index, 2)], preferred_element_type=f32)
+
+        @pl.when(index >= slots)
         def _():
-            for copy in phase_copies(phase):
-                copy.start()
-
-        @pl.when(step == 3 * phase + 2)
+            pl.semaphore_wait(free_sem, 1)
+
+        exchange(index).start()
+
+    fetch(0).start()
+    fetch(1).start()
+    x_copy = pltpu.make_async_copy(x_hbm, y_ref, x_sem)
+    x_copy.start()
+    barrier = pltpu.get_barrier_semaphore()
+    peers = [other] + [(tp, peer) for axis in range(3) for peer in axis_peers(axis)]
+    for peer in peers:
+        pl.semaphore_signal(barrier, inc=1, device_id=peer, device_id_type=MESH)
+    pl.semaphore_wait(barrier, len(peers))
+    for copy in phase_copies(0):
+        copy.start()
+
+    @pl.loop(0, rows // 32)
+    def _(i):
+        here = pl.ds(pl.multiple_of(i * 32, 32), 32)
+        o_buf[here] = o_ref[here]
+
+    @pl.loop(0, 2)
+    def _(index):
+        fetch(index).wait()
+        multiply(index)
+        fetch(index + 2).start()
+
+    x_copy.wait()
+
+    @pl.loop(2, blocks)
+    def _(index):
+        for phase in range(4):
+            @pl.when(index == 3 * phase + 2)
+            def _():
+                value = max_ref[...] if phase == 0 else best[phase - 1]
+                for copy, slot in zip(phase_copies(phase), phase_slots(phase)):
+                    copy.wait()
+                    value = jnp.maximum(value, peer_best[slot])
+                if phase < 3:
+                    best[phase] = value
+                else:
+                    top_ref[...] = value
+
+            if phase:
+                @pl.when(index == 3 * phase)
+                def _():
+                    for copy in phase_copies(phase):
+                        copy.start()
+
+        fetch(index).wait()
+        exchange(index - 2).wait()
+        finish(index - 2)
+        multiply(index)
+
+        @pl.when(index - 2 < blocks - slots)
         def _():
-            value = max_ref[...] if phase == 0 else best[phase - 1]
-            copies = phase_copies(phase)
-            slots = [0] if phase == 0 else [1 + 3 * (phase - 1) + d for d in range(3)]
-            for copy, slot in zip(copies, slots):
-                copy.wait()
-                value = jnp.maximum(value, peer_best[slot])
-            if phase < 3:
-                best[phase] = value
-            else:
-                top_ref[...] = value
-
-    def finish(index):
-        y_ref[...] = (x_ref[...].astype(f32) + (part[lax.rem(index, 3)] + recv[index])).astype(bf16)
-
-    def multiply():
-        part[lax.rem(step, 3)] = jnp.dot(o_ref[...], w_ref[...], preferred_element_type=f32)
-        exchange(step).start()
-
-    @pl.when(step < 2)
-    def _():
-        multiply()
-
-    @pl.when((step >= 2) & (step < blocks))
-    def _():
-        exchange(step - 2).wait()
-        finish(step - 2)
-        multiply()
-
-    @pl.when(step >= blocks)
-    def _():
-        exchange(step - 2).wait()
-        finish(step - 2)
+            pl.semaphore_signal(free_sem, inc=1, device_id=other, device_id_type=MESH)
+
+        @pl.when(index + 2 < blocks)
+        def _():
+            fetch(index + 2).start()
+
+    for index in (blocks - 2, blocks - 1):
+        exchange(index).wait()
+        finish(index)
 
 
 def output_projection(o, w_out, x, local_max):
     rows, depth = o.shape
     dim = w_out.shape[1]
     width = 512
-    blocks = dim // width
-    whole = lambda shape: pl.BlockSpec(shape, lambda j: (0,) * len(shape), pipeline_mode=pl.Buffered(1))
-    late = pl.BlockSpec((rows, width), lambda j: (0, jnp.maximum(j - 2, 0)))
+    slots = 4
+    vmem, hbm = pl.BlockSpec(memory_space=pltpu.VMEM), pl.BlockSpec(memory_space=pltpu.HBM)
     return pl.pallas_call(
-        lambda *refs: output_kernel(blocks, *refs),
-        grid=(blocks + 2,),
-        in_specs=[whole(o.shape), pl.BlockSpec((depth, width), lambda j: (0, jnp.minimum(j, blocks - 1))), late, whole((8, 128))],
-        out_specs=[late, whole((8, 128))],
-        out_shape=[jax.ShapeDtypeStruct((rows, dim), bf16), jax.ShapeDtypeStruct((8, 128), f32)],
+        output_kernel,
+        in_specs=[vmem, hbm, hbm, vmem],
+        out_specs=[vmem, vmem],
+        out_shape=[pltpu.VMEM((rows, dim), bf16), jax.ShapeDtypeStruct((8, 128), f32)],
         scratch_shapes=[
+            pltpu.VMEM(o.shape, bf16),
+            pltpu.VMEM((2, depth, width), bf16),
             pltpu.VMEM((3, rows, width), f32),
-            pltpu.VMEM((blocks, rows, width), f32),
+            pltpu.VMEM((slots, rows, width), f32),
             pltpu.VMEM((3, 8, 128), f32),
             pltpu.VMEM((10, 8, 128), f32),
+            pltpu.SemaphoreType.DMA,
+            pltpu.SemaphoreType.DMA((2,)),
             pltpu.SemaphoreType.DMA((3,)),
-            pltpu.SemaphoreType.DMA((blocks,)),
+            pltpu.SemaphoreType.DMA((slots,)),
             pltpu.SemaphoreType.DMA((10,)),
             pltpu.SemaphoreType.DMA((10,)),
+            pltpu.SemaphoreType.REGULAR,
         ],
-        compiler_params=pltpu.CompilerParams(vmem_limit_bytes=VMEM_MAX, collective_id=0, has_side_effects=True),
+        compiler_params=pltpu.CompilerParams(vmem_limit_bytes=20 * MIB, collective_id=0, has_side_effects=True),
         name="output_projection",
-    )(o, w_out, x, local_max)
-
-
-def clip_kernel(top_ref, wqb_ref, wkvb_ref, nqb_ref, nkvb_ref):
-    group = pl.program_id(0)
-    first = lax.axis_index("tp") * pl.num_programs(0) * GROUP + group * GROUP
+    )(in_vmem(o), in_hbm(w_out), in_hbm(x), in_vmem(local_max))
+
+
+def clip_kernel(top_ref, wqb_ref, wkvb_ref, y_ref, nqb_ref, nkvb_ref, out_hbm, max_ref, y_sem):
+    group, groups = pl.program_id(0), pl.num_programs(0)
+    first = lax.axis_index("tp") * groups * GROUP + group * GROUP
+    y_copy = pltpu.make_async_copy(y_ref, out_hbm, y_sem)
+
+    @pl.when(group == 0)
+    def _():
+        y_copy.start()
+        for i in range(max_ref.shape[0]):
+            max_ref[i] = top_ref[0, i]
 
     def gains(width, first_dim, second_is_clip):
         column = lax.broadcasted_iota(jnp.int32, (1, GROUP * width), 1)
@@ -410,34 +474,46 @@
         clip = CLIP_TAU / jnp.maximum(CLIP_TAU, best)
         return jnp.where(inner < first_dim, jnp.sqrt(clip), clip if second_is_clip else 1.0)
 
-    nqb_ref[...] = (wqb_ref[...].astype(f32) * gains(QK, NOPE, True)).astype(bf16)
-    nkvb_ref[...] = (wkvb_ref[...].astype(f32) * gains(NOPE + VDIM, NOPE, False)).astype(bf16)
-
-
-def clip(top, wqb, wkvb):
+    for src, dst, width, first_dim, second_is_clip in ((wqb_ref, nqb_ref, QK, NOPE, True), (wkvb_ref, nkvb_ref, NOPE + VDIM, NOPE, False)):
+        gain = gains(width, first_dim, second_is_clip)
+        columns = pl.ds(pl.multiple_of(group * GROUP * width, 256), GROUP * width) if second_is_clip else slice(None)
+
+        @pl.loop(0, src.shape[0] // 256)
+        def _(i):
+            here = pl.ds(pl.multiple_of(i * 256, 256), 256)
+            dst[here] = (src[here, columns].astype(f32) * gain).astype(bf16)
+
+    @pl.when(group == groups - 1)
+    def _():
+        y_copy.wait()
+
+
+def clip(top, wqb, wkvb, y, all_heads):
     steps = wqb.shape[1] // (QK * GROUP)
+    vmem = pl.BlockSpec(memory_space=pltpu.VMEM)
     qspec = pl.BlockSpec((wqb.shape[0], GROUP * QK), lambda g: (0, g))
     kvspec = pl.BlockSpec((wkvb.shape[0], GROUP * (NOPE + VDIM)), lambda g: (0, g))
     return pl.pallas_call(
         clip_kernel,
         grid=(steps,),
-        in_specs=[pl.BlockSpec(memory_space=pltpu.SMEM), qspec, kvspec],
-        out_specs=[qspec, kvspec],
-        out_shape=[jax.ShapeDtypeStruct(wqb.shape, bf16), jax.ShapeDtypeStruct(wkvb.shape, bf16)],
-        compiler_params=pltpu.CompilerParams(vmem_limit_bytes=VMEM_MAX),
+        in_specs=[pl.BlockSpec(memory_space=pltpu.SMEM), vmem, kvspec, vmem],
+        out_specs=[qspec, kvspec, pl.BlockSpec(memory_space=pltpu.HBM), pl.BlockSpec(memory_space=pltpu.SMEM)],
+        out_shape=[jax.ShapeDtypeStruct(wqb.shape, bf16), jax.ShapeDtypeStruct(wkvb.shape, bf16), jax.ShapeDtypeStruct(y.shape, bf16), jax.ShapeDtypeStruct((all_heads,), f32)],
+        scratch_shapes=[pltpu.SemaphoreType.DMA],
+        compiler_params=pltpu.CompilerParams(vmem_limit_bytes=10 * MIB),
         name="clip",
-    )(top, wqb, wkvb)
+    )(top, in_vmem(wqb), in_hbm(wkvb), in_vmem(y))
 
 
 def solution(mesh):
     def device_step(hidden, gain_in, gain_q, gain_kv, w_qa, w_kva, w_qb, w_kvb, w_out):
         x = hidden[0]
         tables = rope_tables(x.shape[0])
-        qlat, lat, kr = latents(x, gain_in[None], gain_q[None], gain_kv[None], w_qa, w_kva.T, tables)
-        o, local_max = attention(qlat, lat, kr, tables, w_qb, w_kvb)
+        qlat, lat, kr = latents(x, gain_in[None], gain_q.reshape(-1, 128), gain_kv[None], w_qa, w_kva.T, tables)
+        o, keep_qb, local_max = attention(qlat, lat, kr, tables, w_qb, w_kvb)
         y, top = output_projection(o, w_out, x, local_max)
-        new_qb, new_kvb = clip(top, w_qb, w_kvb)
-        return y[None], top[0, :64], new_qb, new_kvb
+        new_qb, new_kvb, out, logit_max = clip(top, keep_qb, w_kvb, y, mesh.shape["tp"] * o.shape[1] // VDIM)
+        return out[None], logit_max, new_qb, new_kvb
 
     weight_spec = P(None, 'tp')
     return jax.shard_map(device_step, mesh=mesh, in_specs=(P('dp', None, None), P(), P(), P(), P(), P(), weight_spec, weight_spec, P('tp', None)), out_specs=(P('dp', None, None), P(), weight_spec, weight_spec), check_vma=False)

time: 125 us -> 108 us (0.86)
  Pallas kernels: 115 us -> 103 us
  local copies, waits for them, and re-layouts: 8.72 us -> 3.24 us
    pallas_call x2, Pallas kernels: 73.7 us -> 68.6 us  [the longest x1 39 us: output_projection(): pl.pallas_call(output_kernel, in_specs=[vmem, hbm, hbm, vmem], out_specs=...]
    pallas_call x1, Pallas kernels: 19.9 us -> 15 us  [clip(): pl.pallas_call(clip_kernel, grid=(steps,), in_specs=[pl.BlockSpec(memory_...]
    unnamed x1 -> x8, local copies, waits for them, and re-layouts: 6.23 us -> 3.24 us
    pallas_call x1, Pallas kernels: 21.4 us -> 19.4 us  [latents(): pl.pallas_call(latent_kernel, in_specs=[hbm, vmem, vmem, vmem, hbm, hbm,...]
    broadcast_in_dim x1 -> x0, local copies, waits for them, and re-layouts: 1.29 us -> none  [device_step(): gain_q[None]]
where the time goes in v2:
time: 108 us; the launch traced here: 107 us
  Pallas kernels  103 us (95%)
  local copies, waits for them, and re-layouts  3.24 us (3%)
    pallas_call x1, Pallas kernels, output_projection(): pl.pallas_call(output_kernel, in_specs=[vmem, hbm, hbm, vmem], out_specs=...  39 us
    pallas_call x1, Pallas kernels, attention(): pl.pallas_call(attention_kernel, grid=(groups + 1,), in_specs=[vmem, vmem...  29.6 us
    pallas_call x1, Pallas kernels, latents(): pl.pallas_call(latent_kernel, in_specs=[hbm, vmem, vmem, vmem, hbm, hbm,...  19.4 us
    pallas_call x1, Pallas kernels, clip(): pl.pallas_call(clip_kernel, grid=(steps,), in_specs=[pl.BlockSpec(memory_...  15 us
    unnamed x8, local copies, waits for them, and re-layouts  3.24 us

profile of v2, /device:TPU:1, one launch (start us, length us, event | category | flops | bytes accessed | tf_op | source)
XLA Modules:
  0.0 107.1 jit_solution(2031821312237131051)
XLA Ops:
  0.6 0.0 copy-start
  0.6 1.1 %copy-done = f32[3,512,128]{2,1,0:T(8,128)S(1)} copy-done((f32[3,512,128]{2,1,0:T(8,128)S(1)}, f32[3,512,128]{2,1,0:T(8,128)}, u32[]{:S(2)}) %copy-start) | copy-done | bytes 786456
  1.8 0.0 copy-start.1
  1.8 0.7 copy-done.1
  2.5 0.0 copy-start.2
  2.5 0.7 copy-done.2
  3.2 0.0 copy-start.3
  3.2 0.7 copy-done.3
  3.9 19.4 %latents.1 = (bf16[512,1536]{1,0:T(8,128)(2,1)S(1)}, bf16[512,512]{1,0:T(8,128)(2,1)S(1)}, bf16[2,512,128]{2,1,0:T(8,128)(2,1)S(1)}) custom-call(bf16[512,6144]{1,0:T(8,128)(2,1)} %bitcast.9, f32[1,6144]{1,0:T(1,128)S(1)} %bitcast.6, f32[12,128]{1,0:T(8,128)S(1)} %bitcast.7, f32[1,512]{1,0:T(1,128)S(1)} %bitcast.8, bf16[6144,1536]{1,0:T(8,128)(2,1)} %wqa_hbm.1, ...), custom_call_target="tpu_custom_call" | custom-call | tf_op jit(solution)/shard_map/latents/pallas_call | solution.py:158
  23.2 29.6 %attention.1 = (bf16[512,4096]{1,0:T(8,128)(2,1)S(1)}, bf16[1536,6144]{1,0:T(8,128)(2,1)S(1)}, f32[8,128]{1,0:T(8,128)S(1)}) custom-call(bf16[512,1536]{1,0:T(8,128)(2,1)S(1)} %get-tuple-element.16.qlat_ref, bf16[512,512]{1,0:T(8,128)(2,1)S(1)} %get-tuple-element.17.lat_ref, bf16[2,512,128]{2,1,0:T(8,128)(2,1)S(1)} %get-tuple-element.18.kr_ref, ...), custom_call_target="tpu_custom_call" | custom-call | tf_op jit(solution)/shard_map/attention/pallas_call | solution.py:303
  52.9 39.0 %output_projection.1 = (bf16[512,6144]{1,0:T(8,128)(2,1)S(1)}, f32[8,128]{1,0:T(8,128)S(1)}) custom-call(bf16[512,4096]{1,0:T(8,128)(2,1)S(1)} %get-tuple-element.19.o_ref, bf16[4096,6144]{1,0:T(8,128)(2,1)} %w_hbm.1, bf16[512,6144]{1,0:T(8,128)(2,1)} %bitcast.10, f32[8,128]{1,0:T(8,128)S(1)} %get-tuple-element.20.max_ref), custom_call_target="tpu_custom_call" | custom-call | tf_op jit(solution)/shard_map/output_projection/pallas_call | solution.py:432
  91.9 15.0 %clip.1 = (bf16[1536,6144]{1,0:T(8,128)(2,1)}, bf16[512,8192]{1,0:T(8,128)(2,1)}, bf16[512,6144]{1,0:T(8,128)(2,1)}, f32[64]{0:T(128)}) custom-call(f32[8,128]{1,0:T(8,128)S(1)} %get-tuple-element.21.top_ref, bf16[1536,6144]{1,0:T(8,128)(2,1)S(1)} %get-tuple-element.22.wqb_ref, bf16[512,8192]{1,0:T(8,128)(2,1)} %wkvb_ref.3, ...), custom_call_target="tpu_custom_call" | custom-call | tf_op jit(solution)/shard_map/clip/pallas_call | solution.py:496
Async XLA Ops:
  0.6 1.1 %copy-start = (f32[3,512,128]{2,1,0:T(8,128)S(1)}, f32[3,512,128]{2,1,0:T(8,128)}, u32[]{:S(2)}) copy-start(f32[3,512,128]{2,1,0:T(8,128)} %constant.2.clone.tab_ref) | copy-start | bytes 2359300
  1.8 0.7 copy-start.1
  2.5 0.7 copy-start.2
  3.2 0.7 copy-start.3

commit v3 on v2

--- a/solution.py
+++ b/solution.py
@@ -45,7 +45,7 @@
 TILE = 256
 
 
-def latent_kernel(x_hbm, gin_ref, gq_ref, gkv_ref, wqa_hbm, wkva_hbm, tab_ref, qlat_ref, lat_ref, kr_ref, x_ref, n_ref, wq_ref, wkv_ref, wr_ref, full_q, full_kv, rot, scale_ref, x_sem, w_sem, send_sem, recv_sem):
+def latent_kernel(x_hbm, gin_hbm, gq_hbm, gkv_hbm, wqa_hbm, wkva_hbm, tab_hbm, wqb_hbm, qlat_ref, lat_ref, kr_ref, tab_ref, wqb_ref, gin_ref, gq_ref, gkv_ref, g_sem, x_ref, n_ref, wq_ref, wkv_ref, wr_ref, full_q, full_kv, rot, scale_ref, x_sem, w_sem, send_sem, recv_sem):
     rows, dim = x_ref.shape
     tp, dp = lax.axis_index("tp"), lax.axis_index("dp")
     other = (1 - tp, dp)
@@ -56,7 +56,8 @@
     kv_copy = pltpu.make_async_copy(wkva_hbm.at[pl.ds(pl.multiple_of(tp * TILE, TILE), TILE)], wkv_ref, w_sem.at[tiles])
     r_copy = pltpu.make_async_copy(wkva_hbm.at[pl.ds(rank, ROPE)], wr_ref, w_sem.at[tiles + 1])
     q_copies = [pltpu.make_async_copy(wqa_hbm.at[:, pl.ds(pl.multiple_of((tp * tiles + i) * TILE, TILE), TILE)], wq_ref.at[i], w_sem.at[i]) for i in range(tiles)]
-    for copy in [*x_copies, *q_copies, kv_copy, r_copy]:
+    small = [pltpu.make_async_copy(src, dst, g_sem.at[i]) for i, (src, dst) in enumerate(((gin_hbm, gin_ref), (gq_hbm, gq_ref), (gkv_hbm, gkv_ref), (tab_hbm, tab_ref), (wqb_hbm, wqb_ref)))]
+    for copy in [*x_copies, *small[:3]]:
         copy.start()
     barrier = pltpu.get_barrier_semaphore()
     pl.semaphore_signal(barrier, inc=1, device_id=other, device_id_type=MESH)
@@ -88,12 +89,18 @@
     upper, lower = slice(0, half), slice(half, rows)
 
     measure(0)
+    q_copies[0].start()
+    q_copies[1].start()
+    for copy in small[:3]:
+        copy.wait()
 
     @pl.loop(0, half // 32)
     def _(i):
         normalize(pl.ds(pl.multiple_of(i * 32, 32), 32))
 
     measure(1)
+    for copy in [q_copies[2], kv_copy, r_copy, small[3]]:
+        copy.start()
     q_copies[0].wait()
     q_copies[1].wait()
     for j in range(2):
@@ -106,6 +113,7 @@
     sends = [send(full_q, tp * tiles + j, j) for j in range(2)]
     for copy in sends:
         copy.start()
+    small[4].start()
     q_copies[2].wait()
     for part in (upper, lower):
         full_q[tp * tiles + 2, part] = jnp.dot(n_ref[part], wq_ref[2], preferred_element_type=f32)
@@ -136,7 +144,7 @@
         for j, a in enumerate(pieces):
             qlat_ref[here, j * TILE:j * TILE + TILE] = (a * scale * jnp.concatenate([gq_ref[2 * j:2 * j + 1], gq_ref[2 * j + 1:2 * j + 2]], axis=1)).astype(bf16)
 
-    for copy in sends[3:]:
+    for copy in [*sends[3:], small[3]]:
         copy.wait()
     for r in range(0, rows, 64):
         here = slice(r, r + 64)
@@ -148,19 +156,24 @@
         key = turn(rot[r // half, r % half:r % half + 64], [tab_ref[i, here] for i in range(3)])
         kr_ref[0, here] = key.astype(bf16)
         kr_ref[1, here] = pltpu.roll(key, 64, 1).astype(bf16)
-
-
-def latents(x, gin, gq, gkv, wqa, wkva, tables):
+    small[4].wait()
+
+
+def latents(x, gin, gq, gkv, wqa, wkva, tables, wqb):
     rows, dim = x.shape
     q_rank, rank = wqa.shape[1], gkv.shape[1]
     tiles = q_rank // (2 * TILE)
     vmem, hbm = pl.BlockSpec(memory_space=pltpu.VMEM), pl.BlockSpec(memory_space=pltpu.HBM)
     return pl.pallas_call(
         latent_kernel,
-        in_specs=[hbm, vmem, vmem, vmem, hbm, hbm, vmem],
-        out_specs=[vmem, vmem, vmem],
-        out_shape=[pltpu.VMEM((rows, q_rank), bf16), pltpu.VMEM((rows, rank), bf16), pltpu.VMEM((2, rows, 128), bf16)],
+        in_specs=[hbm] * 8,
+        out_specs=[vmem] * 5,
+        out_shape=[pltpu.VMEM((rows, q_rank), bf16), pltpu.VMEM((rows, rank), bf16), pltpu.VMEM((2, rows, 128), bf16), pltpu.VMEM(tables.shape, f32), pltpu.VMEM(wqb.shape, bf16)],
         scratch_shapes=[
+            pltpu.VMEM(gin.shape, f32),
+            pltpu.VMEM(gq.shape, f32),
+            pltpu.VMEM(gkv.shape, f32),
+            pltpu.SemaphoreType.DMA((5,)),
             pltpu.VMEM((rows, dim), bf16),
             pltpu.VMEM((rows, dim), bf16),
             pltpu.VMEM((tiles, dim, TILE), bf16),
@@ -177,13 +190,13 @@
         ],
         compiler_params=pltpu.CompilerParams(vmem_limit_bytes=32 * MIB, collective_id=1, has_side_effects=True),
         name="latents",
-    )(in_hbm(x), gin, gq, gkv, in_hbm(wqa), in_hbm(wkva), tables)
-
-
-BLOCK, CHUNK = 256, 32
-
-
-def attention_kernel(qlat_ref, lat_ref, kr_ref, tab_ref, wqb_hbm, wkvb_ref, o_ref, wqb_ref, max_ref, w_sem, mirror, *scratch):
+    )(*(in_hbm(a) for a in (x, gin, gq, gkv, wqa, wkva, tables, wqb)))
+
+
+BLOCK, CHUNK, WIDTH = 256, 32, 512
+
+
+def attention_kernel(qlat_ref, lat_ref, kr_ref, tab_ref, wqb_ref, wkvb_ref, wout_hbm, o_ref, max_ref, head_ref, w_sem, mirror, *scratch):
     step, steps = pl.program_id(0), pl.num_programs(0)
     sets = (scratch[0:3], scratch[3:6])
     raws, probs = scratch[6:10], scratch[10:14]
@@ -191,18 +204,15 @@
     rows = qlat_ref.shape[0]
     lane = lax.broadcasted_iota(jnp.int32, (rows, 128), 1)
 
-    def fetch(group):
-        columns = pl.ds(pl.multiple_of(group * (GROUP * QK), 256), GROUP * QK)
-        return pltpu.make_async_copy(wqb_hbm.at[:, columns], wqb_ref.at[:, columns], w_sem.at[group])
-
-    @pl.when(step == 0)
-    def _():
-        for group in range(heads // GROUP):
-            fetch(group).start()
-
-    @pl.when(step < steps - 1)
-    def _():
-        fetch(step).wait()
+    head_copy = pltpu.make_async_copy(wout_hbm.at[:, pl.ds(0, head_ref.shape[1])], head_ref, w_sem)
+
+    @pl.when(step == 1)
+    def _():
+        head_copy.start()
+
+    @pl.when(step == steps - 1)
+    def _():
+        head_copy.wait()
 
     @pl.when(step == 0)
     def _():
@@ -294,7 +304,7 @@
             attend(sets[1], h)
 
 
-def attention(qlat, lat, kr, tables, wqb, wkvb):
+def attention(qlat, lat, kr, tables, wqb, wkvb, w_out):
     rows = qlat.shape[0]
     heads = wqb.shape[1] // QK
     groups = heads // GROUP
@@ -303,13 +313,13 @@
     return pl.pallas_call(
         attention_kernel,
         grid=(groups + 1,),
-        in_specs=[vmem, vmem, vmem, vmem, hbm, pl.BlockSpec((wkvb.shape[0], GROUP * 256), lambda g: (0, jnp.minimum(g, groups - 1)))],
+        in_specs=[vmem, vmem, vmem, vmem, vmem, pl.BlockSpec((wkvb.shape[0], GROUP * 256), lambda g: (0, jnp.minimum(g, groups - 1))), hbm],
         out_specs=[vmem, vmem, vmem],
-        out_shape=[pltpu.VMEM((rows, heads * VDIM), bf16), pltpu.VMEM(wqb.shape, bf16), pltpu.VMEM((8, 128), f32)],
-        scratch_shapes=[pltpu.SemaphoreType.DMA((groups,)), pltpu.VMEM(tables.shape, f32)] + buffers + buffers + [pltpu.VMEM((BLOCK, (1 + i % 2) * BLOCK), f32) for i in range(4)] + [pltpu.VMEM((BLOCK, (1 + i % 2) * BLOCK), bf16) for i in range(4)],
+        out_shape=[pltpu.VMEM((rows, heads * VDIM), bf16), pltpu.VMEM((8, 128), f32), pltpu.VMEM((w_out.shape[0], WIDTH), bf16)],
+        scratch_shapes=[pltpu.SemaphoreType.DMA, pltpu.VMEM(tables.shape, f32)] + buffers + buffers + [pltpu.VMEM((BLOCK, (1 + i % 2) * BLOCK), f32) for i in range(4)] + [pltpu.VMEM((BLOCK, (1 + i % 2) * BLOCK), bf16) for i in range(4)],
         compiler_params=pltpu.CompilerParams(vmem_limit_bytes=15 * MIB),
         name="attention",
-    )(in_vmem(qlat), in_vmem(lat), in_vmem(kr), tables, in_hbm(wqb), in_hbm(wkvb))
+    )(in_vmem(qlat), in_vmem(lat), in_vmem(kr), in_vmem(tables), in_vmem(wqb), in_hbm(wkvb), in_hbm(w_out))
 
 
 def axis_peers(axis):
@@ -319,7 +329,7 @@
     return [dp + (lax.rem(here + d, 4) - here) * stride for d in (1, 2, 3)]
 
 
-def output_kernel(o_ref, w_hbm, x_hbm, max_ref, y_ref, top_ref, o_buf, w_buf, part, recv, best, peer_best, x_sem, w_sem, send_sem, recv_sem, max_send, max_recv, free_sem):
+def output_kernel(o_ref, head_ref, w_hbm, x_hbm, max_ref, y_ref, top_ref, o_buf, w_buf, part, recv, best, peer_best, x_sem, w_sem, send_sem, recv_sem, max_send, max_recv, free_sem):
     slots, rows, width = recv.shape
     blocks = y_ref.shape[1] // width
     tp, dp = lax.axis_index("tp"), lax.axis_index("dp")
@@ -351,16 +361,6 @@
             here = slice(r, r + 32)
             y_ref[here, columns] = (y_ref[here, columns].astype(f32) + (part[lax.rem(index, 3), here] + recv[lax.rem(index, slots), here])).astype(bf16)
 
-    def multiply(index):
-        part[lax.rem(index, 3)] = jnp.dot(o_buf[...], w_buf[lax.rem(index, 2)], preferred_element_type=f32)
-
-        @pl.when(index >= slots)
-        def _():
-            pl.semaphore_wait(free_sem, 1)
-
-        exchange(index).start()
-
-    fetch(0).start()
     fetch(1).start()
     x_copy = pltpu.make_async_copy(x_hbm, y_ref, x_sem)
     x_copy.start()
@@ -377,12 +377,14 @@
         here = pl.ds(pl.multiple_of(i * 32, 32), 32)
         o_buf[here] = o_ref[here]
 
-    @pl.loop(0, 2)
-    def _(index):
-        fetch(index).wait()
-        multiply(index)
-        fetch(index + 2).start()
-
+    for index in range(2):
+        if index:
+            fetch(index).wait()
+        else:
+            fetch(2).start()
+        part[index] = jnp.dot(o_buf[...], w_buf[1] if index else head_ref[...], preferred_element_type=f32)
+        exchange(index).start()
+    fetch(3).start()
     x_copy.wait()
 
     @pl.loop(2, blocks)
@@ -408,7 +410,13 @@
         fetch(index).wait()
         exchange(index - 2).wait()
         finish(index - 2)
-        multiply(index)
+        part[lax.rem(index, 3)] = jnp.dot(o_buf[...], w_buf[lax.rem(index, 2)], preferred_element_type=f32)
+
+        @pl.when(index >= slots)
+        def _():
+            pl.semaphore_wait(free_sem, 1)
+
+        exchange(index).start()
 
         @pl.when(index - 2 < blocks - slots)
         def _():
@@ -423,15 +431,15 @@
         finish(index)
 
 
-def output_projection(o, w_out, x, local_max):
+def output_projection(o, head, w_out, x, local_max):
     rows, depth = o.shape
     dim = w_out.shape[1]
-    width = 512
+    width = WIDTH
     slots = 4
     vmem, hbm = pl.BlockSpec(memory_space=pltpu.VMEM), pl.BlockSpec(memory_space=pltpu.HBM)
     return pl.pallas_call(
         output_kernel,
-        in_specs=[vmem, hbm, hbm, vmem],
+        in_specs=[vmem, vmem, hbm, hbm, vmem],
         out_specs=[vmem, vmem],
         out_shape=[pltpu.VMEM((rows, dim), bf16), jax.ShapeDtypeStruct((8, 128), f32)],
         scratch_shapes=[
@@ -451,7 +459,7 @@
         ],
         compiler_params=pltpu.CompilerParams(vmem_limit_bytes=20 * MIB, collective_id=0, has_side_effects=True),
         name="output_projection",
-    )(in_vmem(o), in_hbm(w_out), in_hbm(x), in_vmem(local_max))
+    )(in_vmem(o), in_vmem(head), in_hbm(w_out), in_hbm(x), in_vmem(local_max))
 
 
 def clip_kernel(top_ref, wqb_ref, wkvb_ref, y_ref, nqb_ref, nkvb_ref, out_hbm, max_ref, y_sem):
@@ -508,10 +516,9 @@
 def solution(mesh):
     def device_step(hidden, gain_in, gain_q, gain_kv, w_qa, w_kva, w_qb, w_kvb, w_out):
         x = hidden[0]
-        tables = rope_tables(x.shape[0])
-        qlat, lat, kr = latents(x, gain_in[None], gain_q.reshape(-1, 128), gain_kv[None], w_qa, w_kva.T, tables)
-        o, keep_qb, local_max = attention(qlat, lat, kr, tables, w_qb, w_kvb)
-        y, top = output_projection(o, w_out, x, local_max)
+        qlat, lat, kr, tables, keep_qb = latents(x, gain_in[None], gain_q.reshape(-1, 128), gain_kv[None], w_qa, w_kva.T, rope_tables(x.shape[0]), w_qb)
+        o, local_max, head = attention(qlat, lat, kr, tables, keep_qb, w_kvb, w_out)
+        y, top = output_projection(o, head, w_out, x, local_max)
         new_qb, new_kvb, out, logit_max = clip(top, keep_qb, w_kvb, y, mesh.shape["tp"] * o.shape[1] // VDIM)
         return out[None], logit_max, new_qb, new_kvb
 

time: 108 us -> 99 us (0.917)
  Pallas kernels: 103 us -> 97.9 us
  local copies, waits for them, and re-layouts: 3.24 us -> 0 us
    pallas_call x1, Pallas kernels: 29.6 us -> 26.3 us  [attention(): pl.pallas_call(attention_kernel, grid=(groups + 1,), in_specs=[vmem, vmem...]
    unnamed x8 -> x0, local copies, waits for them, and re-layouts: 3.24 us -> none
    pallas_call x2, Pallas kernels: 58.4 us -> 56.5 us  [the longest x1 38.9 us: output_projection(): pl.pallas_call(output_kernel, in_specs=[vmem, vmem, hbm, hbm, vmem], out_...]
where the time goes in v3:
time: 99 us; the launch traced here: 98.7 us
  Pallas kernels  97.9 us (99%)
    pallas_call x1, Pallas kernels, output_projection(): pl.pallas_call(output_kernel, in_specs=[vmem, vmem, hbm, hbm, vmem], out_...  38.9 us
    pallas_call x1, Pallas kernels, attention(): pl.pallas_call(attention_kernel, grid=(groups + 1,), in_specs=[vmem, vmem...  26.3 us
    pallas_call x1, Pallas kernels, latents(): pl.pallas_call(latent_kernel, in_specs=[hbm] * 8, out_specs=[vmem] * 5, o...  17.7 us
    pallas_call x1, Pallas kernels, clip(): pl.pallas_call(clip_kernel, grid=(steps,), in_specs=[pl.BlockSpec(memory_...  15 us

profile of v3, /device:TPU:1, one launch (start us, length us, event | category | flops | bytes accessed | tf_op | source)
XLA Modules:
  0.0 98.7 jit_solution(16225264419411769015)
XLA Ops:
  0.6 17.7 %latents.1 = (bf16[512,1536]{1,0:T(8,128)(2,1)S(1)}, bf16[512,512]{1,0:T(8,128)(2,1)S(1)}, bf16[2,512,128]{2,1,0:T(8,128)(2,1)S(1)}, f32[3,512,128]{2,1,0:T(8,128)S(1)}, bf16[1536,6144]{1,0:T(8,128)(2,1)S(1)}) custom-call(bf16[512,6144]{1,0:T(8,128)(2,1)} %bitcast.6, f32[1,6144]{1,0:T(1,128)} %bitcast.9, f32[12,128]{1,0:T(8,128)} %bitcast.10, ...), custom_call_target="tpu_custom_call" | custom-call | tf_op jit(solution)/shard_map/latents/pallas_call | solution.py:167
  18.3 26.3 %attention.1 = (bf16[512,4096]{1,0:T(8,128)(2,1)S(1)}, f32[8,128]{1,0:T(8,128)S(1)}, bf16[4096,512]{1,0:T(8,128)(2,1)S(1)}) custom-call(bf16[512,1536]{1,0:T(8,128)(2,1)S(1)} %get-tuple-element.18.qlat_ref, bf16[512,512]{1,0:T(8,128)(2,1)S(1)} %get-tuple-element.19.lat_ref, bf16[2,512,128]{2,1,0:T(8,128)(2,1)S(1)} %get-tuple-element.20.kr_ref, ...), custom_call_target="tpu_custom_call" | custom-call | tf_op jit(solution)/shard_map/attention/pallas_call | solution.py:313
  44.6 38.9 %output_projection.1 = (bf16[512,6144]{1,0:T(8,128)(2,1)S(1)}, f32[8,128]{1,0:T(8,128)S(1)}) custom-call(bf16[512,4096]{1,0:T(8,128)(2,1)S(1)} %get-tuple-element.23.o_ref, bf16[4096,512]{1,0:T(8,128)(2,1)S(1)} %get-tuple-element.24.head_ref, bf16[4096,6144]{1,0:T(8,128)(2,1)} %w_hbm.1, bf16[512,6144]{1,0:T(8,128)(2,1)} %bitcast.7, ...), custom_call_target="tpu_custom_call" | custom-call | tf_op jit(solution)/shard_map/output_projection/pallas_call | solution.py:440
  83.5 15.0 %clip.1 = (bf16[1536,6144]{1,0:T(8,128)(2,1)}, bf16[512,8192]{1,0:T(8,128)(2,1)}, bf16[512,6144]{1,0:T(8,128)(2,1)}, f32[64]{0:T(128)}) custom-call(f32[8,128]{1,0:T(8,128)S(1)} %get-tuple-element.26.top_ref, bf16[1536,6144]{1,0:T(8,128)(2,1)S(1)} %get-tuple-element.22.wqb_ref, bf16[512,8192]{1,0:T(8,128)(2,1)} %wkvb_ref.3, ...), custom_call_target="tpu_custom_call" | custom-call | tf_op jit(solution)/shard_map/clip/pallas_call | solution.py:504

commit v4 on v3

--- a/solution.py
+++ b/solution.py
@@ -71,7 +71,7 @@
         x_copies[2 * part].wait()
         x_copies[2 * part + 1].wait()
 
-        @pl.loop(0, half // 32)
+        @pl.loop(0, half // 32, unroll=4)
         def _(i):
             here = pl.ds(pl.multiple_of(part * half + i * 32, 32), 32)
             total = jnp.zeros((32, 256), f32)
@@ -94,7 +94,7 @@
     for copy in small[:3]:
         copy.wait()
 
-    @pl.loop(0, half // 32)
+    @pl.loop(0, half // 32, unroll=2)
     def _(i):
         normalize(pl.ds(pl.multiple_of(i * 32, 32), 32))
 
@@ -135,7 +135,7 @@
     for copy in sends[:3]:
         copy.wait()
 
-    @pl.loop(0, rows // 32)
+    @pl.loop(0, rows // 32, unroll=4)
     def _(i):
         here = pl.ds(pl.multiple_of(i * 32, 32), 32)
         pieces = [full_q[j, here] for j in range(2 * tiles)]
@@ -331,16 +331,20 @@
 
 def output_kernel(o_ref, head_ref, w_hbm, x_hbm, max_ref, y_ref, top_ref, o_buf, w_buf, part, recv, best, peer_best, x_sem, w_sem, send_sem, recv_sem, max_send, max_recv, free_sem):
     slots, rows, width = recv.shape
-    blocks = y_ref.shape[1] // width
+    blocks, depth = y_ref.shape[1] // width, w_buf.shape[0]
     tp, dp = lax.axis_index("tp"), lax.axis_index("dp")
     other = (1 - tp, dp)
 
     def fetch(index):
-        slot = lax.rem(index, 2)
+        slot = lax.rem(index, depth)
         return pltpu.make_async_copy(w_hbm.at[:, pl.ds(pl.multiple_of(index * width, width), width)], w_buf.at[slot], w_sem.at[slot])
 
+    def x_copy(index):
+        columns = pl.ds(pl.multiple_of(index * width, width), width)
+        return pltpu.make_async_copy(x_hbm.at[:, columns], y_ref.at[:, columns], x_sem.at[index])
+
     def exchange(index):
-        slot, place = lax.rem(index, 3), lax.rem(index, slots)
+        slot, place = lax.rem(index, 2), lax.rem(index, slots)
         return pltpu.make_async_remote_copy(src_ref=part.at[slot], dst_ref=recv.at[place], send_sem=send_sem.at[slot], recv_sem=recv_sem.at[place], device_id=other, device_id_type=MESH)
 
     def spread(phase, slot, device):
@@ -359,11 +363,10 @@
         columns = pl.ds(pl.multiple_of(index * width, width), width)
         for r in range(0, rows, 32):
             here = slice(r, r + 32)
-            y_ref[here, columns] = (y_ref[here, columns].astype(f32) + (part[lax.rem(index, 3), here] + recv[lax.rem(index, slots), here])).astype(bf16)
-
-    fetch(1).start()
-    x_copy = pltpu.make_async_copy(x_hbm, y_ref, x_sem)
-    x_copy.start()
+            y_ref[here, columns] = (y_ref[here, columns].astype(f32) + (part[lax.rem(index, 2), here] + recv[lax.rem(index, slots), here])).astype(bf16)
+
+    for index in range(1, depth):
+        fetch(index).start()
     barrier = pltpu.get_barrier_semaphore()
     peers = [other] + [(tp, peer) for axis in range(3) for peer in axis_peers(axis)]
     for peer in peers:
@@ -381,11 +384,11 @@
         if index:
             fetch(index).wait()
         else:
-            fetch(2).start()
+            fetch(depth).start()
         part[index] = jnp.dot(o_buf[...], w_buf[1] if index else head_ref[...], preferred_element_type=f32)
         exchange(index).start()
-    fetch(3).start()
-    x_copy.wait()
+        x_copy(index).start()
+    fetch(depth + 1).start()
 
     @pl.loop(2, blocks)
     def _(index):
@@ -407,10 +410,12 @@
                     for copy in phase_copies(phase):
                         copy.start()
 
+        x_copy(index).start()
         fetch(index).wait()
+        x_copy(index - 2).wait()
         exchange(index - 2).wait()
         finish(index - 2)
-        part[lax.rem(index, 3)] = jnp.dot(o_buf[...], w_buf[lax.rem(index, 2)], preferred_element_type=f32)
+        part[lax.rem(index, 2)] = jnp.dot(o_buf[...], w_buf[lax.rem(index, depth)], preferred_element_type=f32)
 
         @pl.when(index >= slots)
         def _():
@@ -422,11 +427,12 @@
         def _():
             pl.semaphore_signal(free_sem, inc=1, device_id=other, device_id_type=MESH)
 
-        @pl.when(index + 2 < blocks)
+        @pl.when(index + depth < blocks)
         def _():
-            fetch(index + 2).start()
+            fetch(index + depth).start()
 
     for index in (blocks - 2, blocks - 1):
+        x_copy(index).wait()
         exchange(index).wait()
         finish(index)
 
@@ -435,7 +441,7 @@
     rows, depth = o.shape
     dim = w_out.shape[1]
     width = WIDTH
-    slots = 4
+    slots, ring = 4, 3
     vmem, hbm = pl.BlockSpec(memory_space=pltpu.VMEM), pl.BlockSpec(memory_space=pltpu.HBM)
     return pl.pallas_call(
         output_kernel,
@@ -444,20 +450,20 @@
         out_shape=[pltpu.VMEM((rows, dim), bf16), jax.ShapeDtypeStruct((8, 128), f32)],
         scratch_shapes=[
             pltpu.VMEM(o.shape, bf16),
-            pltpu.VMEM((2, depth, width), bf16),
-            pltpu.VMEM((3, rows, width), f32),
+            pltpu.VMEM((ring, depth, width), bf16),
+            pltpu.VMEM((2, rows, width), f32),
             pltpu.VMEM((slots, rows, width), f32),
             pltpu.VMEM((3, 8, 128), f32),
             pltpu.VMEM((10, 8, 128), f32),
-            pltpu.SemaphoreType.DMA,
+            pltpu.SemaphoreType.DMA((dim // width,)),
+            pltpu.SemaphoreType.DMA((ring,)),
             pltpu.SemaphoreType.DMA((2,)),
-            pltpu.SemaphoreType.DMA((3,)),
             pltpu.SemaphoreType.DMA((slots,)),
             pltpu.SemaphoreType.DMA((10,)),
             pltpu.SemaphoreType.DMA((10,)),
             pltpu.SemaphoreType.REGULAR,
         ],
-        compiler_params=pltpu.CompilerParams(vmem_limit_bytes=20 * MIB, collective_id=0, has_side_effects=True),
+        compiler_params=pltpu.CompilerParams(vmem_limit_bytes=23 * MIB, collective_id=0, has_side_effects=True),
         name="output_projection",
     )(in_vmem(o), in_vmem(head), in_hbm(w_out), in_hbm(x), in_vmem(local_max))
 

time: 99 us -> 97.9 us (0.989)
  Pallas kernels: 97.9 us -> 96.8 us
where the time goes in v4:
time: 97.9 us; the launch traced here: 97.6 us
  Pallas kernels  96.8 us (99%)
    pallas_call x1, Pallas kernels, output_projection(): pl.pallas_call(output_kernel, in_specs=[vmem, vmem, hbm, hbm, vmem], out_...  38.2 us
    pallas_call x1, Pallas kernels, attention(): pl.pallas_call(attention_kernel, grid=(groups + 1,), in_specs=[vmem, vmem...  26.3 us
    pallas_call x1, Pallas kernels, latents(): pl.pallas_call(latent_kernel, in_specs=[hbm] * 8, out_specs=[vmem] * 5, o...  17.2 us
    pallas_call x1, Pallas kernels, clip(): pl.pallas_call(clip_kernel, grid=(steps,), in_specs=[pl.BlockSpec(memory_...  15 us

profile of v4, /device:TPU:1, one launch (start us, length us, event | category | flops | bytes accessed | tf_op | source)
XLA Modules:
  0.0 97.6 jit_solution(9523643839448117899)
XLA Ops:
  0.6 17.2 %latents.1 = (bf16[512,1536]{1,0:T(8,128)(2,1)S(1)}, bf16[512,512]{1,0:T(8,128)(2,1)S(1)}, bf16[2,512,128]{2,1,0:T(8,128)(2,1)S(1)}, f32[3,512,128]{2,1,0:T(8,128)S(1)}, bf16[1536,6144]{1,0:T(8,128)(2,1)S(1)}) custom-call(bf16[512,6144]{1,0:T(8,128)(2,1)} %bitcast.6, f32[1,6144]{1,0:T(1,128)} %bitcast.9, f32[12,128]{1,0:T(8,128)} %bitcast.10, ...), custom_call_target="tpu_custom_call" | custom-call | tf_op jit(solution)/shard_map/latents/pallas_call | solution.py:167
  17.9 26.3 %attention.1 = (bf16[512,4096]{1,0:T(8,128)(2,1)S(1)}, f32[8,128]{1,0:T(8,128)S(1)}, bf16[4096,512]{1,0:T(8,128)(2,1)S(1)}) custom-call(bf16[512,1536]{1,0:T(8,128)(2,1)S(1)} %get-tuple-element.18.qlat_ref, bf16[512,512]{1,0:T(8,128)(2,1)S(1)} %get-tuple-element.19.lat_ref, bf16[2,512,128]{2,1,0:T(8,128)(2,1)S(1)} %get-tuple-element.20.kr_ref, ...), custom_call_target="tpu_custom_call" | custom-call | tf_op jit(solution)/shard_map/attention/pallas_call | solution.py:313
  44.2 38.2 %output_projection.1 = (bf16[512,6144]{1,0:T(8,128)(2,1)S(1)}, f32[8,128]{1,0:T(8,128)S(1)}) custom-call(bf16[512,4096]{1,0:T(8,128)(2,1)S(1)} %get-tuple-element.23.o_ref, bf16[4096,512]{1,0:T(8,128)(2,1)S(1)} %get-tuple-element.24.head_ref, bf16[4096,6144]{1,0:T(8,128)(2,1)} %w_hbm.1, bf16[512,6144]{1,0:T(8,128)(2,1)} %bitcast.7, ...), custom_call_target="tpu_custom_call" | custom-call | tf_op jit(solution)/shard_map/output_projection/pallas_call | solution.py:446
  82.4 15.0 %clip.1 = (bf16[1536,6144]{1,0:T(8,128)(2,1)}, bf16[512,8192]{1,0:T(8,128)(2,1)}, bf16[512,6144]{1,0:T(8,128)(2,1)}, f32[64]{0:T(128)}) custom-call(f32[8,128]{1,0:T(8,128)S(1)} %get-tuple-element.26.top_ref, bf16[1536,6144]{1,0:T(8,128)(2,1)S(1)} %get-tuple-element.22.wqb_ref, bf16[512,8192]{1,0:T(8,128)(2,1)} %wkvb_ref.3, ...), custom_call_target="tpu_custom_call" | custom-call | tf_op jit(solution)/shard_map/clip/pallas_call | solution.py:510

commit v5 on v4

--- a/solution.py
+++ b/solution.py
@@ -329,7 +329,7 @@
     return [dp + (lax.rem(here + d, 4) - here) * stride for d in (1, 2, 3)]
 
 
-def output_kernel(o_ref, head_ref, w_hbm, x_hbm, max_ref, y_ref, top_ref, o_buf, w_buf, part, recv, best, peer_best, x_sem, w_sem, send_sem, recv_sem, max_send, max_recv, free_sem):
+def output_kernel(o_ref, head_ref, w_hbm, x_hbm, max_ref, y_ref, top_ref, o_buf, w_buf, part, recv, best, peer_best, x_sem, w_sem, send_sem, recv_sem, max_send, max_recv, half_send, half_recv, free_sem):
     slots, rows, width = recv.shape
     blocks, depth = y_ref.shape[1] // width, w_buf.shape[0]
     tp, dp = lax.axis_index("tp"), lax.axis_index("dp")
@@ -359,9 +359,9 @@
         devices = [other] if phase == 0 else [(tp, peer) for peer in axis_peers(phase - 1)]
         return [spread(phase, slot, device) for slot, device in zip(phase_slots(phase), devices)]
 
-    def finish(index):
+    def finish(index, start=0, stop=None):
         columns = pl.ds(pl.multiple_of(index * width, width), width)
-        for r in range(0, rows, 32):
+        for r in range(start, stop or rows, 32):
             here = slice(r, r + 32)
             y_ref[here, columns] = (y_ref[here, columns].astype(f32) + (part[lax.rem(index, 2), here] + recv[lax.rem(index, slots), here])).astype(bf16)
 
@@ -371,9 +371,6 @@
     peers = [other] + [(tp, peer) for axis in range(3) for peer in axis_peers(axis)]
     for peer in peers:
         pl.semaphore_signal(barrier, inc=1, device_id=peer, device_id_type=MESH)
-    pl.semaphore_wait(barrier, len(peers))
-    for copy in phase_copies(0):
-        copy.start()
 
     @pl.loop(0, rows // 32)
     def _(i):
@@ -386,29 +383,35 @@
         else:
             fetch(depth).start()
         part[index] = jnp.dot(o_buf[...], w_buf[1] if index else head_ref[...], preferred_element_type=f32)
+        if index == 0:
+            pl.semaphore_wait(barrier, len(peers))
+            for copy in phase_copies(0):
+                copy.start()
         exchange(index).start()
         x_copy(index).start()
     fetch(depth + 1).start()
 
-    @pl.loop(2, blocks)
+    def gather_max(phase):
+        value = max_ref[...] if phase == 0 else best[phase - 1]
+        for copy, slot in zip(phase_copies(phase), phase_slots(phase)):
+            copy.wait()
+            value = jnp.maximum(value, peer_best[slot])
+        if phase < 3:
+            best[phase] = value
+        else:
+            top_ref[...] = value
+
+    @pl.loop(2, blocks - 1)
     def _(index):
-        for phase in range(4):
+        for phase in range(3):
             @pl.when(index == 3 * phase + 2)
             def _():
-                value = max_ref[...] if phase == 0 else best[phase - 1]
-                for copy, slot in zip(phase_copies(phase), phase_slots(phase)):
-                    copy.wait()
-                    value = jnp.maximum(value, peer_best[slot])
-                if phase < 3:
-                    best[phase] = value
-                else:
-                    top_ref[...] = value
-
-            if phase:
-                @pl.when(index == 3 * phase)
-                def _():
-                    for copy in phase_copies(phase):
-                        copy.start()
+                gather_max(phase)
+
+            @pl.when(index == 3 * phase + 3)
+            def _():
+                for copy in phase_copies(phase + 1):
+                    copy.start()
 
         x_copy(index).start()
         fetch(index).wait()
@@ -431,10 +434,33 @@
         def _():
             fetch(index + depth).start()
 
-    for index in (blocks - 2, blocks - 1):
-        x_copy(index).wait()
-        exchange(index).wait()
-        finish(index)
+    last, half = blocks - 1, rows // 2
+
+    def exchange_half(i):
+        here = pl.ds(i * half, half)
+        return pltpu.make_async_remote_copy(
+            src_ref=part.at[last % 2, here], dst_ref=recv.at[last % slots, here], send_sem=half_send.at[i], recv_sem=half_recv.at[i], device_id=other, device_id_type=MESH
+        )
+
+    gather_max(3)
+    x_copy(last).start()
+    fetch(last).wait()
+    x_copy(last - 2).wait()
+    exchange(last - 2).wait()
+    finish(last - 2)
+    for i in range(2):
+        here = slice(i * half, i * half + half)
+        part[last % 2, here] = jnp.dot(o_buf[here], w_buf[last % depth], preferred_element_type=f32)
+        if i == 0:
+            pl.semaphore_wait(free_sem, 1)
+        exchange_half(i).start()
+    x_copy(last - 1).wait()
+    exchange(last - 1).wait()
+    finish(last - 1)
+    x_copy(last).wait()
+    for i in range(2):
+        exchange_half(i).wait()
+        finish(last, i * half, i * half + half)
 
 
 def output_projection(o, head, w_out, x, local_max):
@@ -461,6 +487,8 @@
             pltpu.SemaphoreType.DMA((slots,)),
             pltpu.SemaphoreType.DMA((10,)),
             pltpu.SemaphoreType.DMA((10,)),
+            pltpu.SemaphoreType.DMA((2,)),
+            pltpu.SemaphoreType.DMA((2,)),
             pltpu.SemaphoreType.REGULAR,
         ],
         compiler_params=pltpu.CompilerParams(vmem_limit_bytes=23 * MIB, collective_id=0, has_side_effects=True),

time: 97.9 us -> 94.6 us (0.966)
  Pallas kernels: 96.8 us -> 93.4 us
    pallas_call x1, Pallas kernels: 38.2 us -> 34.9 us  [output_projection(): pl.pallas_call(output_kernel, in_specs=[vmem, vmem, hbm, hbm, vmem], out_...]
where the time goes in v5:
time: 94.6 us; the launch traced here: 94.3 us
  Pallas kernels  93.4 us (99%)
    pallas_call x1, Pallas kernels, output_projection(): pl.pallas_call(output_kernel, in_specs=[vmem, vmem, hbm, hbm, vmem], out_...  34.9 us
    pallas_call x1, Pallas kernels, attention(): pl.pallas_call(attention_kernel, grid=(groups + 1,), in_specs=[vmem, vmem...  26.3 us
    pallas_call x1, Pallas kernels, latents(): pl.pallas_call(latent_kernel, in_specs=[hbm] * 8, out_specs=[vmem] * 5, o...  17.2 us
    pallas_call x1, Pallas kernels, clip(): pl.pallas_call(clip_kernel, grid=(steps,), in_specs=[pl.BlockSpec(memory_...  15 us

profile of v5, /device:TPU:1, one launch (start us, length us, event | category | flops | bytes accessed | tf_op | source)
XLA Modules:
  0.0 94.3 jit_solution(16696538410178351832)
XLA Ops:
  0.6 17.2 %latents.1 = (bf16[512,1536]{1,0:T(8,128)(2,1)S(1)}, bf16[512,512]{1,0:T(8,128)(2,1)S(1)}, bf16[2,512,128]{2,1,0:T(8,128)(2,1)S(1)}, f32[3,512,128]{2,1,0:T(8,128)S(1)}, bf16[1536,6144]{1,0:T(8,128)(2,1)S(1)}) custom-call(bf16[512,6144]{1,0:T(8,128)(2,1)} %bitcast.6, f32[1,6144]{1,0:T(1,128)} %bitcast.9, f32[12,128]{1,0:T(8,128)} %bitcast.10, ...), custom_call_target="tpu_custom_call" | custom-call | tf_op jit(solution)/shard_map/latents/pallas_call | solution.py:167
  17.9 26.3 %attention.1 = (bf16[512,4096]{1,0:T(8,128)(2,1)S(1)}, f32[8,128]{1,0:T(8,128)S(1)}, bf16[4096,512]{1,0:T(8,128)(2,1)S(1)}) custom-call(bf16[512,1536]{1,0:T(8,128)(2,1)S(1)} %get-tuple-element.18.qlat_ref, bf16[512,512]{1,0:T(8,128)(2,1)S(1)} %get-tuple-element.19.lat_ref, bf16[2,512,128]{2,1,0:T(8,128)(2,1)S(1)} %get-tuple-element.20.kr_ref, ...), custom_call_target="tpu_custom_call" | custom-call | tf_op jit(solution)/shard_map/attention/pallas_call | solution.py:313
  44.2 34.9 %output_projection.1 = (bf16[512,6144]{1,0:T(8,128)(2,1)S(1)}, f32[8,128]{1,0:T(8,128)S(1)}) custom-call(bf16[512,4096]{1,0:T(8,128)(2,1)S(1)} %get-tuple-element.23.o_ref, bf16[4096,512]{1,0:T(8,128)(2,1)S(1)} %get-tuple-element.24.head_ref, bf16[4096,6144]{1,0:T(8,128)(2,1)} %w_hbm.1, bf16[512,6144]{1,0:T(8,128)(2,1)} %bitcast.7, ...), custom_call_target="tpu_custom_call" | custom-call | tf_op jit(solution)/shard_map/output_projection/pallas_call | solution.py:472
  79.1 15.0 %clip.1 = (bf16[1536,6144]{1,0:T(8,128)(2,1)}, bf16[512,8192]{1,0:T(8,128)(2,1)}, bf16[512,6144]{1,0:T(8,128)(2,1)}, f32[64]{0:T(128)}) custom-call(f32[8,128]{1,0:T(8,128)S(1)} %get-tuple-element.26.top_ref, bf16[1536,6144]{1,0:T(8,128)(2,1)S(1)} %get-tuple-element.22.wqb_ref, bf16[512,8192]{1,0:T(8,128)(2,1)} %wkvb_ref.3, ...), custom_call_target="tpu_custom_call" | custom-call | tf_op jit(solution)/shard_map/clip/pallas_call | solution.py:538
